TPU v7x, 256 devices: a whole 4x4x8 slice. The times are simulated.
256 devices in a mesh: first: 16 (over y, x), second: 16 (over z, core).
Axes of the slice: x: 4, y: 4, z: 8, core: 2. Of those that a mesh axis runs over, the one named last changes fastest.
Arguments:
- pair_state: bfloat16 [768, 768, 128], P('first', 'second'), may hold values from -6 to 6
- in_gain: float32 [128], replicated, may hold values from 0.25 to 1.75
- left_weight: bfloat16 [128, 128], replicated, may hold values from -0.5 to 0.5
- right_weight: bfloat16 [128, 128], replicated, may hold values from -0.5 to 0.5
- mid_gain: float32 [128], replicated, may hold values from 0.25 to 1.75
- out_weight: bfloat16 [128, 128], replicated, may hold values from -0.5 to 0.5
- out_gate: bfloat16 [128, 128], replicated, may hold values from -0.5 to 0.5
Outputs:
- triangle_out: bfloat16 [768, 768, 128], P('first', 'second')
All inputs are finite; a program needn't handle non-finite values.
Results may differ from a plain program's by a relative error of at most 0.015.
Values may be sent and summed in bfloat16 or wider, within the bound.
A program may use at most 64 MiB of HBM per device.

v0:
```python
import functools

import jax
import jax.numpy as jnp
from jax import lax
from jax.experimental import pallas as pl
from jax.experimental.pallas import tpu as pltpu
from jax.sharding import PartitionSpec as P

MESH = pl.DeviceIdType.MESH
F32 = jnp.float32
BF16 = jnp.bfloat16
CORES = 2
PIECES = 2


def unit_channels(values, channel_gain):
    centred = values - jnp.mean(values, axis=-1, keepdims=True)
    return (
        centred
        * lax.rsqrt(jnp.mean(centred * centred, axis=-1, keepdims=True) + 1e-05)
        * channel_gain
    )


def bit_xor(left, right, count):
    total, bit = 0, 1
    while bit < count:
        total = total + (left // bit % 2 + right // bit % 2) % 2 * bit
        bit *= 2
    return total


def triangle_kernel(
    groups, count, pieces,
    x_hbm, in_gain_hbm, left_weight_hbm, right_weight_hbm, mid_gain_hbm, out_weight_hbm,
    out_gate_hbm, out_ref,
    x_ref, in_gain, left_weight, right_weight, mid_gain, out_weight, out_gate, fetch_sems,
    left_send, left_recv, right_send, right_recv, right_rows, left_f, right_f,
    part_send, part_recv, own_part, gate,
    left_sems, right_send_sems, right_recv_sems, part_send_sems, part_recv_sems,
):
    cols, rows, width = x_ref.shape
    half = rows // CORES
    some = half // pieces
    pairs = rows * cols
    a = lax.axis_index("first")
    b = lax.axis_index("second")
    z, c = b // CORES, b % CORES
    other = 1 - c

    def core_at(first, layer, core):
        return {"first": first, "second": layer * CORES + core}

    barrier = pltpu.get_barrier_semaphore()
    peers = [core_at(a, z, other)]
    for s in range(1, groups):
        peers += [core_at(bit_xor(a, s, groups), z, c), core_at(bit_xor(a, s, groups), z, other)]
        peers.append(core_at(a, bit_xor(z, s, groups), c))
    for peer in peers:
        pl.semaphore_signal(barrier, inc=1, device_id=peer, device_id_type=MESH)

    fetches = [
        pltpu.make_async_copy(src, dst, fetch_sems.at[n])
        for n, (src, dst) in enumerate([
            (x_hbm, x_ref), (in_gain_hbm, in_gain), (right_weight_hbm, right_weight),
            (left_weight_hbm, left_weight), (out_gate_hbm, out_gate),
            (mid_gain_hbm, mid_gain), (out_weight_hbm, out_weight),
        ])
    ]
    for fetch in fetches:
        fetch.start()
    got_x, got_in_gain, got_right, got_left, got_gate, got_mid_gain, got_out = fetches

    got_x.wait()
    got_in_gain.wait()
    values = x_ref[...].astype(F32).reshape(pairs, width)
    ready = unit_channels(values, in_gain[...].reshape(1, width)).astype(BF16)

    got_right.wait()
    right_rows[...] = jnp.dot(ready, right_weight[...], preferred_element_type=F32)
    for p in range(CORES):
        for h in range(pieces):
            for k in range(cols):
                start = k * rows + p * half + h * some
                right_f[p, k * some : (k + 1) * some, :] = right_rows[start : start + some, :]
            right_send[p, h] = right_f[p].astype(BF16)

    pl.semaphore_wait(barrier, len(peers))

    def right_copy(s, h, r):
        core = c if r == 0 else other
        return pltpu.make_async_remote_copy(
            src_ref=right_send.at[core, h],
            dst_ref=right_recv.at[s, h, r],
            send_sem=right_send_sems.at[s, h, r],
            recv_sem=right_recv_sems.at[s, h, r],
            device_id=core_at(bit_xor(a, s, groups), z, core),
            device_id_type=MESH,
        )

    order = [(s, h) for s in (0, groups - 1) for h in range(pieces)]
    order += [(s, h) for h in range(pieces) for s in range(groups - 2, 0, -1)]

    right_copies = []
    for s, h in order:
        for r in range(CORES):
            if s > 0 or r > 0:
                copy = right_copy(s, h, r)
                copy.start()
                right_copies.append(copy)

    got_left.wait()
    left = jnp.dot(ready, left_weight[...], preferred_element_type=F32).astype(BF16)
    left_send[...] = left
    left_f[0] = left.astype(F32)
    left_copy = pltpu.make_async_remote_copy(
        src_ref=left_send,
        dst_ref=left_recv,
        send_sem=left_sems.at[0],
        recv_sem=left_sems.at[1],
        device_id=core_at(a, z, other),
        device_id_type=MESH,
    )
    left_copy.start()

    left_copy.wait_recv()
    left_f[1] = left_recv[...].astype(F32)

    part_copies = []
    for s, h in order:
        if s == 0:
            right_f[0] = right_send[c, h].astype(F32)
        else:
            right_copy(s, h, 0).wait_recv()
            right_f[0] = right_recv[s, h, 0].astype(F32)
        right_copy(s, h, 1).wait_recv()
        right_f[1] = right_recv[s, h, 1].astype(F32)

        def step(k, sums):
            sums = list(sums)
            for r in range(CORES):
                line = left_f[r, pl.ds(pl.multiple_of(k * rows, 8), rows), :]
                for j in range(some):
                    sums[j] = sums[j] + line * right_f[r, pl.ds(k * some + j, 1), :]
            return tuple(sums)

        sums = lax.fori_loop(
            0, cols, step, tuple(jnp.zeros((rows, width), F32) for _ in range(some))
        )
        part = jnp.concatenate(sums, axis=0)
        part_send[s, h] = part.astype(BF16)
        layer = bit_xor(a, s, groups)
        turn = bit_xor(layer, z, groups)
        copy = pltpu.make_async_remote_copy(
            src_ref=part_send.at[s, h],
            dst_ref=part_recv.at[turn, h],
            send_sem=part_send_sems.at[s, h],
            recv_sem=part_recv_sems.at[turn, h],
            device_id=core_at(a, layer, c),
            device_id_type=MESH,
        )

        @pl.when(turn != 0)
        def _():
            copy.start()

        @pl.when(turn == 0)
        def _():
            own_part[h] = part

        part_copies.append((turn, copy))

    got_gate.wait()
    gate[...] = jax.nn.sigmoid(jnp.dot(ready, out_gate[...], preferred_element_type=F32))
    got_mid_gain.wait()
    got_out.wait()
    for h in range(pieces):
        total = own_part[h]
        for t in range(1, groups):
            pltpu.make_async_remote_copy(
                src_ref=part_send.at[0, h],
                dst_ref=part_recv.at[t, h],
                send_sem=part_send_sems.at[0, h],
                recv_sem=part_recv_sems.at[t, h],
                device_id=core_at(a, bit_xor(z, t, groups), c),
                device_id_type=MESH,
            ).wait_recv()
            total = total + part_recv[t, h].astype(F32)

        mixed = (total * count ** (-0.5)).astype(BF16).astype(F32)
        scaled = unit_channels(mixed, mid_gain[...].reshape(1, width)).astype(BF16)
        result = jnp.dot(scaled, out_weight[...], preferred_element_type=F32)
        result = result * gate[h * some * rows : (h + 1) * some * rows, :]
        out_ref[h * some : (h + 1) * some] = result.reshape(some, rows, width).astype(BF16)

    left_copy.wait_send()
    for copy in right_copies:
        copy.wait_send()
    for turn, copy in part_copies:

        @pl.when(turn != 0)
        def _(copy=copy):
            copy.wait_send()


def by_kernel(pair_state, in_gain, left_weight, right_weight, mid_gain, out_weight, out_gate):
    rows, cols, width = pair_state.shape
    groups = lax.axis_size("first")
    count = cols * lax.axis_size("second")
    pairs = rows * cols
    pieces = PIECES if rows // CORES % PIECES == 0 else 1
    some = rows // CORES // pieces
    changed = pl.pallas_call(
        functools.partial(triangle_kernel, groups, count, pieces),
        out_shape=jax.ShapeDtypeStruct((cols, rows, width), BF16),
        in_specs=[pl.BlockSpec(memory_space=pltpu.MemorySpace.HBM)] * 7,
        out_specs=pl.BlockSpec(memory_space=pltpu.VMEM),
        scratch_shapes=[
            pltpu.VMEM((cols, rows, width), BF16),
            pltpu.VMEM((width,), F32),
            pltpu.VMEM(left_weight.shape, BF16),
            pltpu.VMEM(right_weight.shape, BF16),
            pltpu.VMEM((width,), F32),
            pltpu.VMEM(out_weight.shape, BF16),
            pltpu.VMEM(out_gate.shape, BF16),
            pltpu.SemaphoreType.DMA((7,)),
            pltpu.VMEM((pairs, width), BF16),
            pltpu.VMEM((pairs, width), BF16),
            pltpu.VMEM((CORES, pieces, cols * some, width), BF16),
            pltpu.VMEM((groups, pieces, CORES, cols * some, width), BF16),
            pltpu.VMEM((pairs, width), F32),
            pltpu.VMEM((CORES, pairs, width), F32),
            pltpu.VMEM((CORES, cols * some, width), F32),
            pltpu.VMEM((groups, pieces, rows * some, width), BF16),
            pltpu.VMEM((groups, pieces, rows * some, width), BF16),
            pltpu.VMEM((pieces, rows * some, width), F32),
            pltpu.VMEM((pairs, width), F32),
            pltpu.SemaphoreType.DMA((2,)),
            pltpu.SemaphoreType.DMA((groups, pieces, CORES)),
            pltpu.SemaphoreType.DMA((groups, pieces, CORES)),
            pltpu.SemaphoreType.DMA((groups, pieces)),
            pltpu.SemaphoreType.DMA((groups, pieces)),
        ],
        compiler_params=pltpu.CompilerParams(
            collective_id=0, has_side_effects=True, vmem_limit_bytes=8 * 1024 * 1024
        ),
    )(
        *(
            pltpu.with_memory_space_constraint(value, pltpu.MemorySpace.HBM)
            for value in (
                jnp.swapaxes(pair_state, 0, 1),
                in_gain, left_weight, right_weight, mid_gain, out_weight, out_gate,
            )
        )
    )
    return jnp.swapaxes(changed, 0, 1)


def make_factors(pair_in, in_gain, left_weight, right_weight):
    ready = unit_channels(pair_in.astype(jnp.float32), in_gain).astype(jnp.bfloat16)
    ready = lax.optimization_barrier(ready)
    left = jnp.einsum("ijc,cd->ijd", ready, left_weight, preferred_element_type=jnp.float32)
    right = jnp.einsum("ijc,cd->ijd", ready, right_weight, preferred_element_type=jnp.float32)
    return (ready, left.astype(jnp.bfloat16), right.astype(jnp.bfloat16))


def finish_pair(mixed, ready, mid_gain, out_weight, out_gate):
    scaled = unit_channels(mixed.astype(jnp.float32), mid_gain).astype(jnp.bfloat16)
    scaled = lax.optimization_barrier(scaled)
    gate = jax.nn.sigmoid(
        jnp.einsum("ijc,cd->ijd", ready, out_gate, preferred_element_type=jnp.float32)
    )
    return (
        jnp.einsum("ijd,dc->ijc", scaled, out_weight, preferred_element_type=jnp.float32) * gate
    ).astype(jnp.bfloat16)


def by_collectives(pair_state, in_gain, left_weight, right_weight, mid_gain, out_weight, out_gate):
    ready, left, right = make_factors(pair_state, in_gain, left_weight, right_weight)
    count = pair_state.shape[1] * lax.axis_size("second")
    left_lines, right_lines = (
        lax.all_to_all(left, "second", split_axis=2, concat_axis=1, tiled=True),
        lax.all_to_all(right, "second", split_axis=2, concat_axis=1, tiled=True),
    )

    def meet(piece):
        return jnp.einsum("ikd,jkd->ijd", left_lines, piece, preferred_element_type=jnp.float32)

    strip = meet(lax.all_gather(right_lines, "first", axis=0, tiled=True))
    strip = (strip * count ** (-0.5)).astype(jnp.bfloat16)
    mixed = lax.all_to_all(strip, "second", split_axis=1, concat_axis=2, tiled=True)
    return finish_pair(mixed, ready, mid_gain, out_weight, out_gate)


def per_device(pair_state, *rest):
    groups, parts = lax.axis_size("first"), lax.axis_size("second")
    rows, cols, width = pair_state.shape
    fits = (
        parts == CORES * groups
        and groups > 1
        and groups & (groups - 1) == 0
        and rows == CORES * cols
        and rows % 8 == 0
        and rows * cols % 32 == 0
        and rows // 8 * cols <= 48
    )
    return (by_kernel if fits else by_collectives)(pair_state, *rest)


def solution(mesh):
    in_specs = (P("first", "second", None), P(), P(), P(), P(), P(), P())
    out_specs = P("first", "second", None)
    return jax.shard_map(
        per_device, mesh=mesh, in_specs=in_specs, out_specs=out_specs, check_vma=False
    )
```

profile of v0, /device:TPU:1, one launch (start us, length us, event | category | flops | bytes accessed | tf_op | source)
XLA Modules:
  0.0 180.6 jit_solution(738637115696771919)
XLA Ops:
  6.5 1.5 convert_reduce_fusion
  8.1 1.8 fusion.13
  9.9 1.4 fusion.15
  11.3 0.8 copy-done.2
  12.1 0.3 convolution_convert_fusion.1
  12.4 1.0 copy.17
  13.4 2.4 %reshape.39 = bf16[16,2,9216]{2,1,0:T(2,128)(2,1)S(1)} reshape(bf16[128,48,48]{2,1,0:T(8,128)(2,1)S(1)} %bitcast.60) | data formatting | bytes 1179648
  15.8 28.4 %all_to_all.45 = bf16[16,2,9216]{2,1,0:T(2,128)(2,1)S(1)} all-to-all(bf16[16,2,9216]{2,1,0:T(2,128)(2,1)S(1)} %reshape.39), channel_id=1, replica_groups=mesh['first'=16,'second'=16] {'second'}, dimensions={0} | all-to-all | bytes 1179648 | tf_op jit(solution)/shard_map/all_to_all | solution.py:284
  44.2 1.5 reshape.40
  45.8 1.0 copy.19
  46.8 2.3 %all_to_all.36 = bf16[48,768,8]{1,0,2:T(8,128)(2,1)} reshape(bf16[48,16,48,8]{2,1,0,3:T(8,128)(2,1)S(1)} %copy.19) | data formatting | bytes 1179648 | tf_op jit(solution)/shard_map/all_to_all | solution.py:284
  49.1 0.3 convolution_convert_fusion
  49.4 1.0 copy.20
  50.4 2.4 %reshape.41 = bf16[16,2,9216]{2,1,0:T(2,128)(2,1)S(1)} reshape(bf16[128,48,48]{2,1,0:T(8,128)(2,1)S(1)} %bitcast.61) | data formatting | bytes 1179648
  52.8 21.8 %all_to_all.46 = bf16[16,2,9216]{2,1,0:T(2,128)(2,1)S(1)} all-to-all(bf16[16,2,9216]{2,1,0:T(2,128)(2,1)S(1)} %reshape.41), channel_id=1, replica_groups=mesh['first'=16,'second'=16] {'second'}, dimensions={0} | all-to-all | bytes 1179648 | tf_op jit(solution)/shard_map/all_to_all | solution.py:283
  74.5 1.5 reshape.42
  76.1 1.0 copy.22
  77.1 1.6 all_to_all.40
  78.7 47.9 %all-gather.2.cloned.1.call-done = bf16[768,768,8]{1,0,2:T(8,128)(2,1)} async-done(((bf16[48,768,8]{1,0,2:T(8,128)(2,1)}), bf16[768,768,8]{1,0,2:T(8,128)(2,1)}) %all-gather.2.cloned.1.call-update) | async-done | bytes 9437200 | tf_op jit(solution)/shard_map/all_gather | solution.py:290
  126.5 6.5 %fusion.12 = bf16[48,768,8]{1,0,2:T(8,128)(2,1)S(1)} fusion(bf16[768,768,8]{1,0,2:T(8,128)(2,1)} %all-gather.2.cloned.1.call-done, bf16[48,768,8]{1,0,2:T(8,128)(2,1)S(1)} %all_to_all.40), kind=kOutput, calls=%fused_computation.22 | convolution fusion | flops 453574656 | bytes 10616832 | tf_op jit(solution)/shard_map/ikd,jkd->ijd/dot_general | solution.py:288
  133.1 1.1 copy.23
  134.2 3.1 %reshape.43 = bf16[16,2,9216]{2,1,0:T(2,128)(2,1)} reshape(bf16[768,8,48]{2,1,0:T(8,128)(2,1)S(1)} %bitcast.62) | data formatting | bytes 1179648
  137.3 7.9 %all-to-all-start.2 = ((bf16[16,2,9216]{2,1,0:T(2,128)(2,1)}), bf16[16,2,9216]{2,1,0:T(2,128)(2,1)S(1)}, u32[]{:S(2)}, u32[]{:S(2)}) async-start(bf16[16,2,9216]{2,1,0:T(2,128)(2,1)} %reshape.43), calls=%async_computation.2 | async-start | bytes 1179648 | tf_op jit(solution)/shard_map/all_to_all | solution.py:292
  145.2 1.5 fusion.9
  146.7 16.8 %all-to-all-done.2 = bf16[16,2,9216]{2,1,0:T(2,128)(2,1)S(1)} async-done(((bf16[16,2,9216]{2,1,0:T(2,128)(2,1)}), bf16[16,2,9216]{2,1,0:T(2,128)(2,1)S(1)}, u32[]{:S(2)}, u32[]{:S(2)}) %all-to-all-start.2) | async-done | bytes 589856 | tf_op jit(solution)/shard_map/all_to_all | solution.py:292
  163.5 2.4 %reshape.44 = bf16[768,8,48]{2,1,0:T(8,128)(2,1)} reshape(bf16[16,2,9216]{2,1,0:T(2,128)(2,1)S(1)} %all-to-all-done.2) | data formatting | bytes 1179648
  166.0 4.1 %copy.24 = f32[48,16,48,8]{2,3,1,0:T(8,128)S(1)} copy(bf16[48,16,48,8]{0,3,2,1:T(8,128)(2,1)} %bitcast.63) | data formatting | bytes 1769472 | tf_op jit(solution)/shard_map/convert_element_type | solution.py:269
  170.0 0.4 bitcast_reduce_fusion
  170.4 0.6 fusion.4
  171.1 0.7 fusion.2
  171.8 0.5 copy-done.5
  172.4 1.4 fusion.10
  (24 shorter events, 0.1 us)
Async XLA Ops:
  6.5 5.6 %copy-start = (bf16[128,128]{1,0:T(8,128)(2,1)S(1)}, bf16[128,128]{1,0:T(8,128)(2,1)}, u32[]{:S(2)}) copy-start(bf16[128,128]{1,0:T(8,128)(2,1)} %param.10) | copy-start | bytes 98308
  6.5 3.3 %copy-start.1 = (bf16[48,48,128]{2,1,0:T(8,128)(2,1)S(1)}, bf16[48,48,128]{2,1,0:T(8,128)(2,1)}, u32[]{:S(2)}) copy-start(bf16[48,48,128]{2,1,0:T(8,128)(2,1)} %param.7) | copy-start | bytes 1769476
  6.5 120.0 %all-gather.2.cloned.1.call-start = ((), (), s32[]{:S(2)}) async-start(), calls=%async_computation.3 | async-start | bytes 10027008 | tf_op jit(solution)/shard_map/all_gather | solution.py:290
  11.3 0.8 copy-start.2
  46.8 2.3 %copy-start.3 = (bf16[48,48,128]{2,1,0:T(8,128)(2,1)S(1)}, bf16[48,48,128]{2,1,0:T(8,128)(2,1)}, u32[]{:S(2)}) copy-start(bf16[48,48,128]{2,1,0:T(8,128)(2,1)} %copy-done.2) | copy-start | bytes 1769476
  46.8 2.3 %copy-start.7 = (bf16[128,128]{1,0:T(8,128)(2,1)S(1)}, bf16[128,128]{1,0:T(8,128)(2,1)}, u32[]{:S(2)}) copy-start(bf16[128,128]{1,0:T(8,128)(2,1)} %param.9) | copy-start | bytes 98308
  134.2 11.1 %copy-start.4 = (bf16[48,48,128]{2,1,0:T(8,128)(2,1)S(1)}, bf16[48,48,128]{2,1,0:T(8,128)(2,1)}, u32[]{:S(2)}) copy-start(bf16[48,48,128]{2,1,0:T(8,128)(2,1)} %copy-done.2) | copy-start | bytes 1769476
  134.2 11.0 %copy-start.9 = (bf16[128,128]{1,0:T(8,128)(2,1)S(1)}, bf16[128,128]{1,0:T(8,128)(2,1)}, u32[]{:S(2)}) copy-start(bf16[128,128]{1,0:T(8,128)(2,1)} %param.13) | copy-start | bytes 98308
  137.3 26.3 %all-to-all-start.2 = ((bf16[16,2,9216]{2,1,0:T(2,128)(2,1)}), bf16[16,2,9216]{2,1,0:T(2,128)(2,1)S(1)}, u32[]{:S(2)}, u32[]{:S(2)}) async-start(bf16[16,2,9216]{2,1,0:T(2,128)(2,1)} %reshape.43), calls=%async_computation.2 | async-start | bytes 1179648 | tf_op jit(solution)/shard_map/all_to_all | solution.py:292
  170.4 0.7 copy-start.8
  171.1 1.3 copy-start.5
  171.1 1.3 copy-start.6
Sparse Core Ops, SparseCore 0:
  49.2 77.2 all-gather.1
where the time goes:
time: 181 us
  waiting for transfers between devices  64.7 us (36%)
  blocking collectives  50.2 us (28%)
  local copies, waits for them, and re-layouts  27.7 us (15%)
  between operations  13.7 us (8%)
  matrix products  9.99 us (6%)
  starting transfers between devices  7.95 us (4%)
  other arithmetic  6.45 us (4%)
    all_gather x1, waiting for transfers between devices, by_collectives(): strip = meet(lax.all_gather(right_lines, 'first', axis=0, tiled=True))  47.9 us
    all_to_all x1, blocking collectives, by_collectives(): lax.all_to_all(right, 'second', split_axis=2, concat_axis=1, tiled=True)  28.4 us
    all_to_all x1, blocking collectives, by_collectives(): lax.all_to_all(left, 'second', split_axis=2, concat_axis=1, tiled=True)  21.8 us
    all_to_all x1, waiting for transfers between devices, by_collectives(): lax.all_to_all(strip, 'second', split_axis=1, concat_axis=2, tiled=True)  16.8 us
    unnamed x26, local copies, waits for them, and re-layouts  14.7 us
    all_to_all x1, starting transfers between devices, by_collectives(): lax.all_to_all(strip, 'second', split_axis=1, concat_axis=2, tiled=True)  7.95 us
    dot_general x1, matrix products, meet(): jnp.einsum('ikd,jkd->ijd', left_lines, piece, preferred_element_type=jnp....  6.53 us
    convert_element_type x1, local copies, waits for them, and re-layouts, finish_pair(): mixed.astype(jnp.float32)  4.06 us
  transfers between devices with their start and end apart: 2, of which 2 were waited for; matrix products, arithmetic and copies ran while one was open for 4% of the time, Pallas kernels for 0%

commit v1 on v0

v1 whole, which is shorter than its diff:
```python
import functools

import jax
import jax.numpy as jnp
from jax import lax
from jax.experimental import pallas as pl
from jax.experimental.pallas import tpu as pltpu
from jax.sharding import PartitionSpec as P

MESH = pl.DeviceIdType.MESH
F32 = jnp.float32
BF16 = jnp.bfloat16
CORES = 2


SIDE = 4
LANES = 128
GROUP = 16


def unit_rows(values, channel_gain):
    centred = values - jnp.mean(values, axis=-1, keepdims=True)
    return (
        centred
        * lax.rsqrt(jnp.mean(centred * centred, axis=-1, keepdims=True) + 1e-05)
        * channel_gain
    )


def turn_lanes(parts):
    count = len(parts)
    wide = LANES // count
    group = lax.broadcasted_iota(jnp.int32, parts[0].shape, 1) // wide
    parts = list(parts)
    step = 1
    while step < count:
        low = group // step % 2 == 0
        for n in range(count):
            if n // step % 2 == 0:
                one, two = parts[n], parts[n + step]
                parts[n] = jnp.where(low, one, pltpu.roll(two, step * wide, 1))
                parts[n + step] = jnp.where(low, pltpu.roll(one, LANES - step * wide, 1), two)
        step *= 2
    return parts


def triangle_kernel(
    layers, chips, count,
    x_hbm, in_gain_hbm, left_weight_hbm, right_weight_hbm, mid_gain_hbm, out_weight_hbm,
    out_gate_hbm, out_ref,
    x_ref, in_gain, left_weight, right_weight, mid_gain, out_weight, out_gate, fetch_sems,
    both_weight, ready_ref, gate_ref, turn_ref,
    far_send, far_recv, near_send, left_lines, right_lines,
    mix_send, mix_recv, back_send, back_recv,
    far_sems, left_sems, right_sems, mix_sems, back_sems,
):
    rows, cols, width = x_ref.shape
    parts = rows // GROUP
    a = lax.axis_index("first")
    b = lax.axis_index("second")
    z, c = b // CORES, b % CORES
    other = 1 - c
    y, x = a // SIDE, a % SIDE
    side = a % CORES
    pair = a // CORES

    def core_at(first, layer, core):
        return {"first": first, "second": layer * CORES + core}

    def layer_at(s):
        return lax.rem(z + s, layers)

    def chip_at(dy, dx):
        return lax.rem(y + dy, SIDE) * SIDE + lax.rem(x + dx, SIDE)

    hops = [(dy, dx) for dy in (2, 1, 3, 0) for dx in (2, 1, 3, 0) if (dy, dx) != (0, 0)]
    steps = [4, 3, 5, 2, 6, 1, 7] if layers == 8 else list(range(1, layers))

    barrier = pltpu.get_barrier_semaphore()
    peers = [core_at(a, z, other)]
    peers += [core_at(a, layer_at(s), c) for s in steps]
    for hop in hops:
        peers += [core_at(chip_at(*hop), z, c), core_at(chip_at(*hop), z, other)]
    for peer in peers:
        pl.semaphore_signal(barrier, inc=1, device_id=peer, device_id_type=MESH)

    fetches = [
        pltpu.make_async_copy(src, dst, fetch_sems.at[n])
        for n, (src, dst) in enumerate(
            [(x_hbm.at[pl.ds(p * GROUP, GROUP)], x_ref.at[pl.ds(p * GROUP, GROUP)]) for p in range(parts)]
            + [
                (in_gain_hbm, in_gain), (left_weight_hbm, left_weight),
                (right_weight_hbm, right_weight), (out_gate_hbm, out_gate),
                (mid_gain_hbm, mid_gain), (out_weight_hbm, out_weight),
            ]
        )
    ]
    for fetch in fetches:
        fetch.start()
    for fetch in fetches[parts : parts + 3]:
        fetch.wait()

    both_weight[:width, :] = left_weight[...].astype(F32).T.astype(BF16)
    both_weight[width:, :] = right_weight[...].astype(F32).T.astype(BF16)

    def send(src, dst, sems, at, peer):
        return pltpu.make_async_remote_copy(
            src_ref=src, dst_ref=dst, send_sem=sems.at[0, at], recv_sem=sems.at[1, at],
            device_id=peer, device_id_type=MESH,
        )

    def settle(like, sems, way, at):
        pltpu.make_async_copy(like, like, sems.at[way, at]).wait()

    def send_far(f, p):
        for s in steps:
            to = layer_at(s)
            send(
                far_send.at[f, p, to], far_recv.at[f, p, z], far_sems, f * parts + p,
                core_at(a, to, c),
            ).start()

    block = GROUP * GROUP
    for p in range(parts):
        fetches[p].wait()
        values = x_ref[p * GROUP : (p + 1) * GROUP].astype(F32).reshape(GROUP * cols, width)
        ready = unit_rows(values, in_gain[...].reshape(1, width)).astype(BF16)
        ready = ready.reshape(GROUP, parts, GROUP, width)
        for h in range(parts):
            piece = ready[:, h].reshape(block, width)
            ready_ref[h, p * block : (p + 1) * block, :] = piece
            made = lax.dot_general(
                both_weight[...], piece, (((1,), (1,)), ((), ())), preferred_element_type=F32
            ).astype(BF16)
            for f in range(2):
                far_send[f, p, :, :, h * block : (h + 1) * block] = made[
                    f * width : (f + 1) * width
                ].reshape(layers, GROUP, block)
        if p == 0:
            pl.semaphore_wait(barrier, len(peers))
        send_far(0, p)
        for f in range(2):
            far_recv[f, p, z] = far_send[f, p, z]
    for p in range(parts):
        send_far(1, p)

    fetches[parts + 3].wait()
    for h in range(parts):
        gate_ref[h] = jax.nn.sigmoid(
            jnp.dot(ready_ref[h], out_gate[...], preferred_element_type=F32)
        )

    halves = GROUP // layers

    def regroup(f, p):
        def body(h, carry):
            for e in range(halves):
                lanes = pl.ds(pl.multiple_of((h * halves + e) * LANES, LANES), LANES)
                lines = turn_lanes([far_recv[f, p, n, :, lanes].astype(F32) for n in range(layers)])
                for n in range(layers):
                    at = (e * layers + n) * GROUP
                    turn_ref[at : at + GROUP, :] = lines[n]
            lanes = pl.ds(pl.multiple_of(h * LANES, LANES), LANES)
            for d in range(GROUP):
                line = turn_ref[pl.ds(d, GROUP, stride=GROUP), :]
                near_send[f, p, d, :, lanes] = line.astype(BF16)
            return carry

        lax.fori_loop(0, parts, body, 0)

    for p in range(parts):
        settle(far_recv.at[0, p, pl.ds(0, layers - 1)], far_sems, 1, p)
        regroup(0, p)
        mine = c * chips + a
        for hop in hops:
            to = chip_at(*hop)
            for core in (c, other):
                send(
                    near_send.at[0, p, to], left_lines.at[p, mine], left_sems, p,
                    core_at(to, z, core),
                ).start()
        send(
            near_send.at[0, p, a], left_lines.at[p, mine], left_sems, p, core_at(a, z, other)
        ).start()
        left_lines[p, mine] = near_send[0, p, a]

    def give_right(p):
        settle(far_recv.at[1, p, pl.ds(0, layers - 1)], far_sems, 1, parts + p)
        regroup(1, p)
        mine = c * layers + pair
        for hop in hops:
            to = chip_at(*hop)
            send(
                near_send.at[1, p, to], right_lines.at[p, mine], right_sems, p,
                core_at(to, z, side),
            ).start()

        @pl.when(c == side)
        def _():
            right_lines[p, mine] = near_send[1, p, a]

        @pl.when(c != side)
        def _():
            send(
                near_send.at[1, p, a], right_lines.at[p, mine], right_sems, p,
                core_at(a, z, other),
            ).start()

    def meet(p):
        if p == 0:
            for q in range(parts):
                settle(left_lines.at[q, pl.ds(0, CORES * chips - 1)], left_sems, 1, q)

        @pl.when(c == side)
        def _():
            settle(right_lines.at[p, pl.ds(0, chips - 1)], right_sems, 1, p)

        @pl.when(c != side)
        def _():
            settle(right_lines.at[p], right_sems, 1, p)

        deep = near_send.shape[-1]
        for q in range(parts):
            total = None
            for core in range(CORES):
                left = left_lines[q, core * chips : (core + 1) * chips].reshape(chips * GROUP, deep)
                right = right_lines[p, core * layers : (core + 1) * layers].reshape(LANES, deep)
                term = lax.dot_general(
                    left, right, (((1,), (1,)), ((), ())), preferred_element_type=F32
                )
                total = term if total is None else total + term
            mixed = (total * count ** (-0.5)).astype(BF16)
            mix_send[p, :, q] = mixed.reshape(chips, GROUP, LANES)
        for hop in hops:
            to = chip_at(*hop)
            send(mix_send.at[p, to], mix_recv.at[p, a], mix_sems, p, core_at(to, z, c)).start()
        mix_recv[p, a] = mix_send[p, a]

    def give_back(p):
        settle(mix_recv.at[p, pl.ds(0, chips - 1)], mix_sems, 1, p)

        def body(q, carry):
            for d in range(GROUP):
                turn_ref[d * GROUP : (d + 1) * GROUP, :] = mix_recv[p, d, q].astype(F32)
            for e in range(halves):
                lines = turn_lanes([
                    turn_ref[pl.ds(e * layers + n, GROUP, stride=GROUP), :] for n in range(layers)
                ])
                lanes = pl.ds(pl.multiple_of((q * halves + e) * LANES, LANES), LANES)
                for n in range(layers):
                    back_send[p, n, :, lanes] = lines[n].astype(BF16)
            return carry

        lax.fori_loop(0, parts, body, 0)
        for s in steps:
            to = layer_at(s)
            send(back_send.at[p, to], back_recv.at[p, z], back_sems, p, core_at(a, to, c)).start()
        back_recv[p, z] = back_send[p, z]

    def finish(p):
        settle(back_recv.at[p, pl.ds(0, layers - 1)], back_sems, 1, p)
        mixed = back_recv[p].reshape(width, rows * GROUP).astype(F32)
        centred = mixed - jnp.mean(mixed, axis=0, keepdims=True)
        scaled = (
            centred
            * lax.rsqrt(jnp.mean(centred * centred, axis=0, keepdims=True) + 1e-05)
            * mid_gain[...]
        ).astype(BF16)
        result = lax.dot_general(
            scaled, out_weight[...], (((0,), (0,)), ((), ())), preferred_element_type=F32
        )
        result = (result * gate_ref[p]).astype(BF16)
        out_ref[:, p * GROUP : (p + 1) * GROUP, :] = result.reshape(rows, GROUP, width)

    give_right(0)
    for p in range(1, parts):
        give_right(p)
        meet(p - 1)
        if p > 1:
            give_back(p - 2)
    meet(parts - 1)
    fetches[parts + 4].wait()
    fetches[parts + 5].wait()
    for p in range(max(parts - 2, 0), parts):
        give_back(p)
    for p in range(parts):
        finish(p)

    for f in range(2):
        for p in range(parts):
            settle(far_send.at[f, p, pl.ds(0, layers - 1)], far_sems, 0, f * parts + p)
    for p in range(parts):
        settle(left_lines.at[p, pl.ds(0, CORES * chips - 1)], left_sems, 0, p)

        @pl.when(c == side)
        def _(p=p):
            settle(right_lines.at[p, pl.ds(0, chips - 1)], right_sems, 0, p)

        @pl.when(c != side)
        def _(p=p):
            settle(right_lines.at[p], right_sems, 0, p)

        settle(mix_send.at[p, pl.ds(0, chips - 1)], mix_sems, 0, p)
        settle(back_send.at[p, pl.ds(0, layers - 1)], back_sems, 0, p)


def by_kernel(pair_state, in_gain, left_weight, right_weight, mid_gain, out_weight, out_gate):
    rows, cols, width = pair_state.shape
    chips = lax.axis_size("first")
    layers = lax.axis_size("second") // CORES
    count = cols * lax.axis_size("second")
    parts = rows // GROUP
    lanes = parts * GROUP * GROUP
    deep = parts * LANES
    changed = pl.pallas_call(
        functools.partial(triangle_kernel, layers, chips, count),
        out_shape=jax.ShapeDtypeStruct((rows, cols, width), BF16),
        in_specs=[pl.BlockSpec(memory_space=pltpu.MemorySpace.HBM)] * 7,
        out_specs=pl.BlockSpec(memory_space=pltpu.VMEM),
        scratch_shapes=[
            pltpu.VMEM((rows, cols, width), BF16),
            pltpu.VMEM((width,), F32),
            pltpu.VMEM(left_weight.shape, BF16),
            pltpu.VMEM(right_weight.shape, BF16),
            pltpu.VMEM((width, 1), F32),
            pltpu.VMEM(out_weight.shape, BF16),
            pltpu.VMEM(out_gate.shape, BF16),
            pltpu.SemaphoreType.DMA((parts + 6,)),
            pltpu.VMEM((2 * width, width), BF16),
            pltpu.VMEM((parts, rows * GROUP, width), BF16),
            pltpu.VMEM((parts, rows * GROUP, width), F32),
            pltpu.VMEM((GROUP * GROUP, LANES), F32),
            pltpu.VMEM((2, parts, layers, GROUP, lanes), BF16),
            pltpu.VMEM((2, parts, layers, GROUP, lanes), BF16),
            pltpu.VMEM((2, parts, chips, GROUP, deep), BF16),
            pltpu.VMEM((parts, CORES * chips, GROUP, deep), BF16),
            pltpu.VMEM((parts, CORES * layers, GROUP, deep), BF16),
            pltpu.VMEM((parts, chips, parts, GROUP, LANES), BF16),
            pltpu.VMEM((parts, chips, parts, GROUP, LANES), BF16),
            pltpu.VMEM((parts, layers, GROUP, rows * GROUP), BF16),
            pltpu.VMEM((parts, layers, GROUP, rows * GROUP), BF16),
            pltpu.SemaphoreType.DMA((2, 2 * parts)),
            pltpu.SemaphoreType.DMA((2, parts)),
            pltpu.SemaphoreType.DMA((2, parts)),
            pltpu.SemaphoreType.DMA((2, parts)),
            pltpu.SemaphoreType.DMA((2, parts)),
        ],
        compiler_params=pltpu.CompilerParams(
            collective_id=0, has_side_effects=True, vmem_limit_bytes=32 * 1024 * 1024
        ),
    )(
        *(
            pltpu.with_memory_space_constraint(value, pltpu.MemorySpace.HBM)
            for value in (
                pair_state, in_gain, left_weight, right_weight, mid_gain.reshape(width, 1),
                out_weight, out_gate,
            )
        )
    )
    return changed


def unit_channels(values, channel_gain):
    centred = values - jnp.mean(values, axis=-1, keepdims=True)
    return (
        centred
        * lax.rsqrt(jnp.mean(centred * centred, axis=-1, keepdims=True) + 1e-05)
        * channel_gain
    )


def make_factors(pair_in, in_gain, left_weight, right_weight):
    ready = unit_channels(pair_in.astype(jnp.float32), in_gain).astype(jnp.bfloat16)
    ready = lax.optimization_barrier(ready)
    left = jnp.einsum("ijc,cd->ijd", ready, left_weight, preferred_element_type=jnp.float32)
    right = jnp.einsum("ijc,cd->ijd", ready, right_weight, preferred_element_type=jnp.float32)
    return (ready, left.astype(jnp.bfloat16), right.astype(jnp.bfloat16))


def finish_pair(mixed, ready, mid_gain, out_weight, out_gate):
    scaled = unit_channels(mixed.astype(jnp.float32), mid_gain).astype(jnp.bfloat16)
    scaled = lax.optimization_barrier(scaled)
    gate = jax.nn.sigmoid(
        jnp.einsum("ijc,cd->ijd", ready, out_gate, preferred_element_type=jnp.float32)
    )
    return (
        jnp.einsum("ijd,dc->ijc", scaled, out_weight, preferred_element_type=jnp.float32) * gate
    ).astype(jnp.bfloat16)


def by_collectives(pair_state, in_gain, left_weight, right_weight, mid_gain, out_weight, out_gate):
    ready, left, right = make_factors(pair_state, in_gain, left_weight, right_weight)
    count = pair_state.shape[1] * lax.axis_size("second")
    left_lines, right_lines = (
        lax.all_to_all(left, "second", split_axis=2, concat_axis=1, tiled=True),
        lax.all_to_all(right, "second", split_axis=2, concat_axis=1, tiled=True),
    )

    def meet(piece):
        return jnp.einsum("ikd,jkd->ijd", left_lines, piece, preferred_element_type=jnp.float32)

    strip = meet(lax.all_gather(right_lines, "first", axis=0, tiled=True))
    strip = (strip * count ** (-0.5)).astype(jnp.bfloat16)
    mixed = lax.all_to_all(strip, "second", split_axis=1, concat_axis=2, tiled=True)
    return finish_pair(mixed, ready, mid_gain, out_weight, out_gate)


def per_device(pair_state, *rest):
    groups, parts = lax.axis_size("first"), lax.axis_size("second")
    rows, cols, width = pair_state.shape
    left_out = rest[1].shape[1]
    fits = (
        groups == SIDE * SIDE
        and parts == CORES * 8
        and width == GROUP * 8
        and rows == cols
        and rows % GROUP == 0
        and left_out == width
    )
    return (by_kernel if fits else by_collectives)(pair_state, *rest)


def solution(mesh):
    in_specs = (P("first", "second", None), P(), P(), P(), P(), P(), P())
    out_specs = P("first", "second", None)
    return jax.shard_map(
        per_device, mesh=mesh, in_specs=in_specs, out_specs=out_specs, check_vma=False
    )
```

time: 181 us -> 61.6 us (0.34)
  waiting for transfers between devices: 64.7 us -> 0 us
  Pallas kernels: 0 us -> 59.3 us
  blocking collectives: 50.2 us -> 0 us
  local copies, waits for them, and re-layouts: 27.7 us -> 2.21 us
  between operations: 13.7 us -> 0.01 us
  matrix products: 9.99 us -> 0 us
  starting transfers between devices: 7.95 us -> 0 us
  other arithmetic: 6.45 us -> 0 us
    pallas_call x0 -> x1, Pallas kernels: none -> 59.3 us  [by_kernel(): pl.pallas_call(functools.partial(triangle_kernel, layers, chips, count),...]
    all_to_all x2 -> x0, blocking collectives: 50.2 us -> none  [the longest x1 28.4 us: by_collectives(): lax.all_to_all(right, 'second', split_axis=2, concat_axis=1, tiled=True)]
    all_gather x1 -> x0, waiting for transfers between devices: 47.9 us -> none  [by_collectives(): strip = meet(lax.all_gather(right_lines, 'first', axis=0, tiled=True))]
    all_to_all x1 -> x0, waiting for transfers between devices: 16.8 us -> none  [by_collectives(): lax.all_to_all(strip, 'second', split_axis=1, concat_axis=2, tiled=True)]
    unnamed x26 -> x3, local copies, waits for them, and re-layouts: 14.7 us -> 1.47 us
    dot_general x5 -> x0, matrix products: 9.99 us -> none  [the longest x1 6.53 us: meet(): jnp.einsum('ikd,jkd->ijd', left_lines, piece, preferred_element_type=jnp....]
    all_to_all x1 -> x0, starting transfers between devices: 7.95 us -> none  [by_collectives(): lax.all_to_all(strip, 'second', split_axis=1, concat_axis=2, tiled=True)]
    convert_element_type x4 -> x0, local copies, waits for them, and re-layouts: 7.08 us -> none  [the longest x1 4.06 us: finish_pair(): mixed.astype(jnp.float32)]
  transfers between devices with their start and end apart: 2 -> 0, of which waited for: 2 -> 0; matrix products, arithmetic and copies ran while one was open for 4% -> 0% of each run, Pallas kernels for 0% -> 0%
where the time goes in v1:
time: 61.6 us; the launch traced here: 61.5 us
  Pallas kernels  59.3 us (96%)
  local copies, waits for them, and re-layouts  2.21 us (4%)
    pallas_call x1, Pallas kernels, by_kernel(): pl.pallas_call(functools.partial(triangle_kernel, layers, chips, count),...  59.3 us
    unnamed x3, local copies, waits for them, and re-layouts  1.47 us

profile of v1, /device:TPU:1, one launch (start us, length us, event | category | flops | bytes accessed | tf_op | source)
XLA Modules:
  0.0 61.5 jit_solution(11021637264493269313)
XLA Ops:
  0.0 0.0 copy-start
  0.0 0.7 %copy-done = f32[128]{0:T(128)S(1)} copy-done((f32[128]{0:T(128)S(1)}, f32[128]{0:T(128)}, u32[]{:S(2)}) %copy-start) | copy-done | bytes 536
  0.7 0.7 %copy.8.mid_gain_hbm = f32[128,1]{1,0:T(8,128)} copy(f32[128,1]{0,1:T(1,128)S(1)} %bitcast.1) | data formatting | bytes 1024 | tf_op jit(solution)/shard_map/reshape | solution.py:355
  1.4 59.3 %shard_map.73 = bf16[48,48,128]{2,1,0:T(8,128)(2,1)S(1)} custom-call(bf16[48,48,128]{2,1,0:T(8,128)(2,1)} %x_hbm.1, f32[128]{0:T(128)} %in_gain_hbm.1, bf16[128,128]{1,0:T(8,128)(2,1)} %left_weight_hbm.1, bf16[128,128]{1,0:T(8,128)(2,1)} %right_weight_hbm.1, f32[128,1]{1,0:T(8,128)} %copy.8.mid_gain_hbm, bf16[128,128]{1,0:T(8,128)(2,1)} %out_weight_hbm.1, ...), custom_call_target="tpu_custom_call" | custom-call | tf_op jit(solution)/shard_map/pallas_call | solution.py:315
  60.7 0.8 %copy.10 = bf16[48,48,128]{2,1,0:T(8,128)(2,1)} copy(bf16[48,48,128]{2,1,0:T(8,128)(2,1)S(1)} %shard_map.73) | data formatting | bytes 1179648
Async XLA Ops:
  0.0 0.7 %copy-start = (f32[128]{0:T(128)S(1)}, f32[128]{0:T(128)}, u32[]{:S(2)}) copy-start(f32[128]{0:T(128)} %param.11) | copy-start | bytes 1540

commit v2 on v1

v2 whole, which is shorter than its diff:
```python
import functools

import jax
import jax.numpy as jnp
from jax import lax
from jax.experimental import pallas as pl
from jax.experimental.pallas import tpu as pltpu
from jax.sharding import PartitionSpec as P

MESH = pl.DeviceIdType.MESH
F32 = jnp.float32
BF16 = jnp.bfloat16
CORES = 2


SIDE = 4
LANES = 128
GROUP = 16
UNIT = 8
LAG = 3


def unit_rows(values, channel_gain):
    centred = values - jnp.mean(values, axis=-1, keepdims=True)
    return (
        centred
        * lax.rsqrt(jnp.mean(centred * centred, axis=-1, keepdims=True) + 1e-05)
        * channel_gain
    )


def turn_lanes(parts):
    count = len(parts)
    wide = LANES // count
    group = lax.broadcasted_iota(jnp.int32, parts[0].shape, 1) // wide
    parts = list(parts)
    step = 1
    while step < count:
        low = group // step % 2 == 0
        for n in range(count):
            if n // step % 2 == 0:
                one, two = parts[n], parts[n + step]
                parts[n] = jnp.where(low, one, pltpu.roll(two, step * wide, 1))
                parts[n + step] = jnp.where(low, pltpu.roll(one, LANES - step * wide, 1), two)
        step *= 2
    return parts


def triangle_kernel(
    layers, chips, count,
    x_hbm, in_gain_hbm, left_weight_hbm, right_weight_hbm, mid_gain_hbm, out_weight_hbm,
    out_gate_hbm, out_ref,
    x_ref, in_gain, left_weight, right_weight, mid_gain, out_weight, out_gate, fetch_sems,
    both_weight, mid_wide, ready_ref, gate_ref, turn_ref,
    far_right, got_right, far_left, got_left, near_right, right_lines, near_left, left_lines,
    mix_send, mix_recv, back_send, back_recv,
    far_right_sems, far_left_sems, right_sems, left_sems, mix_sems, back_sems,
):
    scope = jax.named_scope
    rows, cols, width = x_ref.shape
    parts = rows // GROUP
    units = rows // UNIT
    halves = GROUP // UNIT
    a = lax.axis_index("first")
    b = lax.axis_index("second")
    z, c = b // CORES, b % CORES
    other = 1 - c
    y, x = a // SIDE, a % SIDE
    side = a % CORES
    pair = a // CORES

    def core_at(first, layer, core):
        return {"first": first, "second": layer * CORES + core}

    def layer_at(s):
        return lax.rem(z + s, layers)

    def chip_at(dy, dx):
        return lax.rem(y + dy, SIDE) * SIDE + lax.rem(x + dx, SIDE)

    hops = [(dy, dx) for dy in (2, 1, 3, 0) for dx in (2, 1, 3, 0) if (dy, dx) != (0, 0)]
    steps = [4, 3, 5, 2, 6, 1, 7]

    barrier = pltpu.get_barrier_semaphore()
    peers = [core_at(a, z, other)]
    peers += [core_at(a, layer_at(s), c) for s in steps]
    for hop in hops:
        peers += [core_at(chip_at(*hop), z, c), core_at(chip_at(*hop), z, other)]
    for peer in peers:
        pl.semaphore_signal(barrier, inc=1, device_id=peer, device_id_type=MESH)

    fetches = [
        pltpu.make_async_copy(src, dst, fetch_sems.at[n])
        for n, (src, dst) in enumerate(
            [(x_hbm.at[pl.ds(p * GROUP, GROUP)], x_ref.at[pl.ds(p * GROUP, GROUP)]) for p in range(parts)]
            + [
                (in_gain_hbm, in_gain), (left_weight_hbm, left_weight),
                (right_weight_hbm, right_weight), (out_gate_hbm, out_gate),
                (mid_gain_hbm, mid_gain), (out_weight_hbm, out_weight),
            ]
        )
    ]
    for fetch in fetches:
        fetch.start()
    for fetch in fetches[parts : parts + 3]:
        fetch.wait()

    both_weight[:width, :] = right_weight[...].astype(F32).T.astype(BF16)
    both_weight[width:, :] = left_weight[...].astype(F32).T.astype(BF16)

    def send(src, dst, sems, at, peer):
        pltpu.make_async_remote_copy(
            src_ref=src, dst_ref=dst, send_sem=sems.at[0, at], recv_sem=sems.at[1, at],
            device_id=peer, device_id_type=MESH,
        ).start()

    def settle(like, sems, way, at):
        with scope("wait"):
            pltpu.make_async_copy(like, like, sems.at[way, at]).wait()

    def send_far(src, dst, sems, p):
        for s in steps:
            to = layer_at(s)
            send(src.at[p, to], dst.at[p, z], sems, p, core_at(a, to, c))

    block = GROUP * GROUP
    for p in range(parts):
        fetches[p].wait()
        values = x_ref[p * GROUP : (p + 1) * GROUP].astype(F32).reshape(GROUP * cols, width)
        ready = unit_rows(values, in_gain[...].reshape(1, width)).astype(BF16)
        ready = ready.reshape(GROUP, parts, GROUP, width)
        for h in range(parts):
            piece = ready[:, h].reshape(block, width)
            made = lax.dot_general(
                both_weight[...], piece, (((1,), (1,)), ((), ())), preferred_element_type=F32
            ).astype(BF16)
            far_right[p, :, :, h * block : (h + 1) * block] = made[:width].reshape(
                layers, GROUP, block
            )
            for e in range(halves):
                u = p * halves + e
                ready_ref[u, h * LANES : (h + 1) * LANES, :] = piece[e * LANES : (e + 1) * LANES]
                far_left[u, :, :, h * LANES : (h + 1) * LANES] = made[
                    width:, e * LANES : (e + 1) * LANES
                ].reshape(layers, GROUP, LANES)
        if p == 0:
            with scope("bar"):
                pl.semaphore_wait(barrier, len(peers))
        send_far(far_right, got_right, far_right_sems, p)
        got_right[p, z] = far_right[p, z]
    for u in range(units):
        send_far(far_left, got_left, far_left_sems, u)
        got_left[u, z] = far_left[u, z]

    with scope("gate"):
        fetches[parts + 3].wait()
        for u in range(units):
            gate_ref[u] = jax.nn.sigmoid(
                jnp.dot(ready_ref[u], out_gate[...], preferred_element_type=F32)
            )
        fetches[parts + 4].wait()
        mid_wide[...] = jnp.broadcast_to(mid_gain[...].reshape(1, width), (width, width)).T
        fetches[parts + 5].wait()

    def give_right(p):
        settle(got_right.at[p, pl.ds(0, layers - 1)], far_right_sems, 1, p)

        def body(h, carry):
            for e in range(halves):
                lanes = pl.ds(pl.multiple_of((h * halves + e) * LANES, LANES), LANES)
                lines = turn_lanes([got_right[p, n, :, lanes].astype(F32) for n in range(layers)])
                for n in range(layers):
                    at = (e * layers + n) * GROUP
                    turn_ref[at : at + GROUP, :] = lines[n]
            lanes = pl.ds(pl.multiple_of(h * LANES, LANES), LANES)
            for d in range(GROUP):
                line = turn_ref[pl.ds(d, GROUP, stride=GROUP), :]
                near_right[p, d, :, lanes] = line.astype(BF16)
            return carry

        with scope("regroup"):
            lax.fori_loop(0, parts, body, 0)
        mine = c * chips + side * layers + pair
        for hop in hops:
            to = chip_at(*hop)
            for core in (c, other):
                send(
                    near_right.at[p, to], right_lines.at[p, mine], right_sems, p,
                    core_at(to, z, core),
                )
        send(near_right.at[p, a], right_lines.at[p, mine], right_sems, p, core_at(a, z, other))
        right_lines[p, mine] = near_right[p, a]

    def give_left(u):
        settle(got_left.at[u, pl.ds(0, layers - 1)], far_left_sems, 1, u)
        with scope("regroup"):
            for h in range(parts):
                lanes = slice(h * LANES, (h + 1) * LANES)
                lines = turn_lanes([got_left[u, n, :, lanes].astype(F32) for n in range(layers)])
                for n in range(UNIT):
                    at = (h * UNIT + n) * GROUP
                    turn_ref[at : at + GROUP, :] = lines[n]
                for d in range(GROUP):
                    line = turn_ref[pl.ds(h * UNIT * GROUP + d, UNIT, stride=GROUP), :]
                    near_left[u, d, :, lanes] = line.astype(BF16)
        mine = c * layers + pair
        for hop in hops:
            to = chip_at(*hop)
            send(
                near_left.at[u, to], left_lines.at[u, mine], left_sems, u, core_at(to, z, side)
            )

        @pl.when(c == side)
        def _():
            left_lines[u, mine] = near_left[u, a]

        @pl.when(c != side)
        def _():
            send(
                near_left.at[u, a], left_lines.at[u, mine], left_sems, u, core_at(a, z, other)
            )

    def settle_some(like, sems, way, at):
        @pl.when(c == side)
        def _():
            settle(like.at[at, pl.ds(0, chips - 1)], sems, way, at)

        @pl.when(c != side)
        def _():
            settle(like.at[at], sems, way, at)

    deep = near_left.shape[-1]

    def meet(u):
        if u == 0:
            for q in range(parts):
                settle(right_lines.at[q, pl.ds(0, CORES * chips - 1)], right_sems, 1, q)
        settle_some(left_lines, left_sems, 1, u)
        with scope("meet"):
            for q in range(parts):
                total = None
                for core in range(CORES):
                    left = left_lines[u, core * layers : (core + 1) * layers]
                    right = right_lines[q, core * chips : (core + 1) * chips]
                    term = lax.dot_general(
                        left.reshape(layers * UNIT, deep), right.reshape(chips * GROUP, deep),
                        (((1,), (1,)), ((), ())), preferred_element_type=F32,
                    )
                    total = term if total is None else total + term
                mixed = (total * count ** (-0.5)).astype(BF16)
                for core in range(CORES):
                    mix_send[u, core * layers : (core + 1) * layers, :, q * LANES : (q + 1) * LANES] = mixed[
                        :, core * LANES : (core + 1) * LANES
                    ].reshape(layers, UNIT, LANES)
        shift = lax.rem(c + x, CORES)

        def give(dy, t):
            to = chip_at(dy, shift + CORES * t)
            half = to // CORES
            return to, half

        for dy in (2, 1, 3, 0):
            for t in (1, 0):
                if (dy, t) != (0, 0):
                    to, half = give(dy, t)
                    for core in range(CORES):
                        send(
                            mix_send.at[u, core * layers + half], mix_recv.at[u, a], mix_sems, u,
                            core_at(to, z, core),
                        )
        to, half = give(0, 0)

        @pl.when(c == side)
        def _():
            send(
                mix_send.at[u, other * layers + half], mix_recv.at[u, a], mix_sems, u,
                core_at(a, z, other),
            )
            mix_recv[u, a] = mix_send[u, c * layers + half]

        @pl.when(c != side)
        def _():
            for core in range(CORES):
                send(
                    mix_send.at[u, core * layers + half], mix_recv.at[u, a], mix_sems, u,
                    core_at(to, z, core),
                )

    def give_back(u):
        settle_some(mix_recv, mix_sems, 1, u)
        with scope("back"):
            for h in range(parts):
                lanes = slice(h * LANES, (h + 1) * LANES)
                for d in range(GROUP):
                    at = (h * GROUP + d) * UNIT
                    turn_ref[at : at + UNIT, :] = mix_recv[u, d, :, lanes].astype(F32)
                lines = turn_lanes([
                    turn_ref[pl.ds(h * GROUP * UNIT + n, GROUP, stride=UNIT), :] for n in range(UNIT)
                ])
                for n in range(layers):
                    back_send[u, n, :, lanes] = lines[n].astype(BF16)
        send_far(back_send, back_recv, back_sems, u)
        back_recv[u, z] = back_send[u, z]

    def finish(u):
        settle(back_recv.at[u, pl.ds(0, layers - 1)], back_sems, 1, u)
        with scope("finish"):
            mixed = back_recv[u].reshape(width, parts * LANES).astype(F32)
            centred = mixed - jnp.mean(mixed, axis=0, keepdims=True)
            scaled = centred * lax.rsqrt(jnp.mean(centred * centred, axis=0, keepdims=True) + 1e-05)
            for h in range(parts):
                some = (scaled[:, h * LANES : (h + 1) * LANES] * mid_wide[...]).astype(BF16)
                result = lax.dot_general(
                    some, out_weight[...], (((0,), (0,)), ((), ())), preferred_element_type=F32
                )
                result = (result * gate_ref[u, h * LANES : (h + 1) * LANES, :]).astype(BF16)
                out_ref[u * UNIT : (u + 1) * UNIT, h * GROUP : (h + 1) * GROUP, :] = result.reshape(
                    UNIT, GROUP, width
                )

    for p in range(parts):
        give_right(p)
    lag = LAG
    plan = []
    for t in range(units + 3 * lag):
        for stage, fn in ((0, give_left), (1, meet), (2, give_back), (3, finish)):
            u = t - stage * lag
            if 0 <= u < units:
                plan.append((fn, u))
    for fn, u in plan:
        fn(u)

    for p in range(parts):
        settle(far_right.at[p, pl.ds(0, layers - 1)], far_right_sems, 0, p)
        settle(right_lines.at[p, pl.ds(0, CORES * chips - 1)], right_sems, 0, p)
    for u in range(units):
        settle(far_left.at[u, pl.ds(0, layers - 1)], far_left_sems, 0, u)
        settle_some(left_lines, left_sems, 0, u)
        settle_some(mix_recv, mix_sems, 0, u)
        settle(back_send.at[u, pl.ds(0, layers - 1)], back_sems, 0, u)


def by_kernel(pair_state, in_gain, left_weight, right_weight, mid_gain, out_weight, out_gate):
    rows, cols, width = pair_state.shape
    chips = lax.axis_size("first")
    layers = lax.axis_size("second") // CORES
    count = cols * lax.axis_size("second")
    parts = rows // GROUP
    units = rows // UNIT
    lanes = parts * GROUP * GROUP
    deep = parts * LANES
    changed = pl.pallas_call(
        functools.partial(triangle_kernel, layers, chips, count),
        out_shape=jax.ShapeDtypeStruct((rows, cols, width), BF16),
        in_specs=[pl.BlockSpec(memory_space=pltpu.MemorySpace.HBM)] * 7,
        out_specs=pl.BlockSpec(memory_space=pltpu.VMEM),
        scratch_shapes=[
            pltpu.VMEM((rows, cols, width), BF16),
            pltpu.VMEM((width,), F32),
            pltpu.VMEM(left_weight.shape, BF16),
            pltpu.VMEM(right_weight.shape, BF16),
            pltpu.VMEM((width,), F32),
            pltpu.VMEM(out_weight.shape, BF16),
            pltpu.VMEM(out_gate.shape, BF16),
            pltpu.SemaphoreType.DMA((parts + 6,)),
            pltpu.VMEM((2 * width, width), BF16),
            pltpu.VMEM((width, width), F32),
            pltpu.VMEM((units, deep, width), BF16),
            pltpu.VMEM((units, deep, width), F32),
            pltpu.VMEM((parts * GROUP * GROUP, LANES), F32),
            pltpu.VMEM((parts, layers, GROUP, lanes), BF16),
            pltpu.VMEM((parts, layers, GROUP, lanes), BF16),
            pltpu.VMEM((units, layers, GROUP, deep), BF16),
            pltpu.VMEM((units, layers, GROUP, deep), BF16),
            pltpu.VMEM((parts, chips, GROUP, deep), BF16),
            pltpu.VMEM((parts, CORES * chips, GROUP, deep), BF16),
            pltpu.VMEM((units, chips, UNIT, deep), BF16),
            pltpu.VMEM((units, chips, UNIT, deep), BF16),
            pltpu.VMEM((units, chips, UNIT, deep), BF16),
            pltpu.VMEM((units, chips, UNIT, deep), BF16),
            pltpu.VMEM((units, layers, GROUP, deep), BF16),
            pltpu.VMEM((units, layers, GROUP, deep), BF16),
            pltpu.SemaphoreType.DMA((2, parts)),
            pltpu.SemaphoreType.DMA((2, units)),
            pltpu.SemaphoreType.DMA((2, parts)),
            pltpu.SemaphoreType.DMA((2, units)),
            pltpu.SemaphoreType.DMA((2, units)),
            pltpu.SemaphoreType.DMA((2, units)),
        ],
        compiler_params=pltpu.CompilerParams(
            collective_id=0, has_side_effects=True, vmem_limit_bytes=32 * 1024 * 1024
        ),
    )(
        *(
            pltpu.with_memory_space_constraint(value, pltpu.MemorySpace.HBM)
            for value in (
                pair_state, in_gain, left_weight, right_weight, mid_gain, out_weight, out_gate,
            )
        )
    )
    return changed


def unit_channels(values, channel_gain):
    centred = values - jnp.mean(values, axis=-1, keepdims=True)
    return (
        centred
        * lax.rsqrt(jnp.mean(centred * centred, axis=-1, keepdims=True) + 1e-05)
        * channel_gain
    )


def make_factors(pair_in, in_gain, left_weight, right_weight):
    ready = unit_channels(pair_in.astype(jnp.float32), in_gain).astype(jnp.bfloat16)
    ready = lax.optimization_barrier(ready)
    left = jnp.einsum("ijc,cd->ijd", ready, left_weight, preferred_element_type=jnp.float32)
    right = jnp.einsum("ijc,cd->ijd", ready, right_weight, preferred_element_type=jnp.float32)
    return (ready, left.astype(jnp.bfloat16), right.astype(jnp.bfloat16))


def finish_pair(mixed, ready, mid_gain, out_weight, out_gate):
    scaled = unit_channels(mixed.astype(jnp.float32), mid_gain).astype(jnp.bfloat16)
    scaled = lax.optimization_barrier(scaled)
    gate = jax.nn.sigmoid(
        jnp.einsum("ijc,cd->ijd", ready, out_gate, preferred_element_type=jnp.float32)
    )
    return (
        jnp.einsum("ijd,dc->ijc", scaled, out_weight, preferred_element_type=jnp.float32) * gate
    ).astype(jnp.bfloat16)


def by_collectives(pair_state, in_gain, left_weight, right_weight, mid_gain, out_weight, out_gate):
    ready, left, right = make_factors(pair_state, in_gain, left_weight, right_weight)
    count = pair_state.shape[1] * lax.axis_size("second")
    left_lines, right_lines = (
        lax.all_to_all(left, "second", split_axis=2, concat_axis=1, tiled=True),
        lax.all_to_all(right, "second", split_axis=2, concat_axis=1, tiled=True),
    )

    def meet(piece):
        return jnp.einsum("ikd,jkd->ijd", left_lines, piece, preferred_element_type=jnp.float32)

    strip = meet(lax.all_gather(right_lines, "first", axis=0, tiled=True))
    strip = (strip * count ** (-0.5)).astype(jnp.bfloat16)
    mixed = lax.all_to_all(strip, "second", split_axis=1, concat_axis=2, tiled=True)
    return finish_pair(mixed, ready, mid_gain, out_weight, out_gate)


def per_device(pair_state, *rest):
    groups, parts = lax.axis_size("first"), lax.axis_size("second")
    rows, cols, width = pair_state.shape
    left_out = rest[1].shape[1]
    fits = (
        groups == SIDE * SIDE
        and parts == CORES * 8
        and width == GROUP * 8
        and rows == cols
        and rows % GROUP == 0
        and left_out == width
    )
    return (by_kernel if fits else by_collectives)(pair_state, *rest)


def solution(mesh):
    in_specs = (P("first", "second", None), P(), P(), P(), P(), P(), P())
    out_specs = P("first", "second", None)
    return jax.shard_map(
        per_device, mesh=mesh, in_specs=in_specs, out_specs=out_specs, check_vma=False
    )
```

time: 61.6 us -> 61.1 us (level)
  local copies, waits for them, and re-layouts: 2.21 us -> 0.82 us
  Pallas kernels: 59.3 us -> 60.2 us
    pallas_call x1, Pallas kernels: 59.3 us -> 60.2 us  [by_kernel(): pl.pallas_call(functools.partial(triangle_kernel, layers, chips, count),...]
    reshape x1 -> x0, local copies, waits for them, and re-layouts: 0.74 us -> none  [by_kernel(): mid_gain.reshape(width, 1)]
    unnamed x3 -> x1, local copies, waits for them, and re-layouts: 1.47 us -> 0.82 us
where the time goes in v2:
time: 61.1 us; the launch traced here: 61 us
  Pallas kernels  60.2 us (99%)
  local copies, waits for them, and re-layouts  0.82 us (1%)
    pallas_call x1, Pallas kernels, by_kernel(): pl.pallas_call(functools.partial(triangle_kernel, layers, chips, count),...  60.2 us

profile of v2, /device:TPU:1, one launch (start us, length us, event | category | flops | bytes accessed | tf_op | source)
XLA Modules:
  0.0 61.0 jit_solution(12944067783538841694)
XLA Ops:
  0.0 60.2 %shard_map.73 = bf16[48,48,128]{2,1,0:T(8,128)(2,1)S(1)} custom-call(bf16[48,48,128]{2,1,0:T(8,128)(2,1)} %x_hbm.1, f32[128]{0:T(128)} %in_gain_hbm.1, bf16[128,128]{1,0:T(8,128)(2,1)} %left_weight_hbm.1, bf16[128,128]{1,0:T(8,128)(2,1)} %right_weight_hbm.1, f32[128]{0:T(128)} %mid_gain_hbm.1, bf16[128,128]{1,0:T(8,128)(2,1)} %out_weight_hbm.1, ...), custom_call_target="tpu_custom_call" | custom-call | tf_op jit(solution)/shard_map/pallas_call | solution.py:352
  60.2 0.8 %copy.9 = bf16[48,48,128]{2,1,0:T(8,128)(2,1)} copy(bf16[48,48,128]{2,1,0:T(8,128)(2,1)S(1)} %shard_map.73) | data formatting | bytes 1179648

commit v3 on v1

v3 whole, which is shorter than its diff:
```python
import functools

import jax
import jax.numpy as jnp
from jax import lax
from jax.experimental import pallas as pl
from jax.experimental.pallas import tpu as pltpu
from jax.sharding import PartitionSpec as P

MESH = pl.DeviceIdType.MESH
F32 = jnp.float32
BF16 = jnp.bfloat16
CORES = 2


SIDE = 4
LANES = 128
GROUP = 16


def unit_rows(values, channel_gain):
    centred = values - jnp.mean(values, axis=-1, keepdims=True)
    return (
        centred
        * lax.rsqrt(jnp.mean(centred * centred, axis=-1, keepdims=True) + 1e-05)
        * channel_gain
    )


def turn_lanes(parts):
    count = len(parts)
    wide = LANES // count
    group = lax.broadcasted_iota(jnp.int32, parts[0].shape, 1) // wide
    parts = list(parts)
    step = 1
    while step < count:
        low = group // step % 2 == 0
        for n in range(count):
            if n // step % 2 == 0:
                one, two = parts[n], parts[n + step]
                parts[n] = jnp.where(low, one, pltpu.roll(two, step * wide, 1))
                parts[n + step] = jnp.where(low, pltpu.roll(one, LANES - step * wide, 1), two)
        step *= 2
    return parts


def triangle_kernel(
    layers, chips, count,
    x_hbm, in_gain_hbm, left_weight_hbm, right_weight_hbm, mid_gain_hbm, out_weight_hbm,
    out_gate_hbm, out_ref,
    x_ref, in_gain, left_weight, right_weight, mid_gain, out_weight, out_gate, fetch_sems,
    left_rows, right_rows, mid_wide, whole_ref, ready_ref, gate_ref, turn_ref,
    far_left, got_left, near_left, left_lines,
    near_right, met_right, far_right, right_lines,
    mix_send, mix_recv, back_send, back_recv,
    far_left_sems, left_sems, near_right_sems, right_sems, mix_sems, back_sems,
):
    scope = jax.named_scope
    rows, cols, width = x_ref.shape
    parts = rows // GROUP
    halves = GROUP // layers
    block = GROUP * GROUP
    a = lax.axis_index("first")
    b = lax.axis_index("second")
    z, c = b // CORES, b % CORES
    other = 1 - c
    y, x = a // SIDE, a % SIDE
    side = a % CORES
    pair = a // CORES

    def core_at(first, layer, core):
        return {"first": first, "second": layer * CORES + core}

    def layer_at(s):
        return lax.rem(z + s, layers)

    def chip_at(dy, dx):
        return lax.rem(y + dy, SIDE) * SIDE + lax.rem(x + dx, SIDE)

    hops = [(dy, dx) for dy in (2, 1, 3, 0) for dx in (2, 1, 3, 0) if (dy, dx) != (0, 0)]
    steps = [4, 3, 5, 2, 6, 1, 7]

    barrier = pltpu.get_barrier_semaphore()
    peers = [core_at(a, z, other)]
    peers += [core_at(a, layer_at(s), c) for s in steps]
    for hop in hops:
        peers += [core_at(chip_at(*hop), z, c), core_at(chip_at(*hop), z, other)]
    for peer in peers:
        pl.semaphore_signal(barrier, inc=1, device_id=peer, device_id_type=MESH)

    fetches = [
        pltpu.make_async_copy(src, dst, fetch_sems.at[n])
        for n, (src, dst) in enumerate(
            [(x_hbm.at[pl.ds(p * GROUP, GROUP)], x_ref.at[pl.ds(p * GROUP, GROUP)]) for p in range(parts)]
            + [
                (in_gain_hbm, in_gain), (left_weight_hbm, left_weight),
                (right_weight_hbm, right_weight), (out_gate_hbm, out_gate),
                (mid_gain_hbm, mid_gain), (out_weight_hbm, out_weight),
            ]
        )
    ]
    for fetch in fetches:
        fetch.start()
    for fetch in fetches[parts : parts + 3]:
        fetch.wait()

    left_rows[...] = left_weight[...].astype(F32).T.astype(BF16)
    turn_ref[:width, :] = right_weight[...].astype(F32).T
    for d in range(chips):
        right_rows[d * layers : (d + 1) * layers, :] = turn_ref[
            pl.ds(d, layers, stride=chips), :
        ].astype(BF16)

    def send(src, dst, sems, at, peer):
        pltpu.make_async_remote_copy(
            src_ref=src, dst_ref=dst, send_sem=sems.at[0, at], recv_sem=sems.at[1, at],
            device_id=peer, device_id_type=MESH,
        ).start()

    def settle(like, sems, way, at):
        with scope("wait"):
            pltpu.make_async_copy(like, like, sems.at[way, at]).wait()

    def settle_some(like, sems, way, at):
        @pl.when(c == side)
        def _():
            settle(like.at[at, pl.ds(0, chips - 1)], sems, way, at)

        @pl.when(c != side)
        def _():
            settle(like.at[at], sems, way, at)

    def send_far(src, dst, sems, p, core):
        for s in steps:
            to = layer_at(s)
            send(src.at[p, to], dst.at[p, z], sems, p, core_at(a, to, core))
        dst[p, z] = src[p, z]

    def project(weight, lines):
        return lax.dot_general(
            weight, lines, (((1,), (1,)), ((), ())), preferred_element_type=F32
        ).astype(BF16)

    def begin(p):
        fetches[p].wait()
        values = x_ref[p * GROUP : (p + 1) * GROUP].astype(F32).reshape(GROUP * cols, width)
        ready = unit_rows(values, in_gain[...].reshape(1, width))
        whole_ref[p] = ready
        ready = ready.astype(BF16).reshape(GROUP, parts, GROUP, width)
        for h in range(parts):
            piece = ready[:, h].reshape(block, width)
            ready_ref[h, p * block : (p + 1) * block, :] = piece
            far_left[p, :, :, h * block : (h + 1) * block] = project(
                left_rows[...], piece
            ).reshape(layers, GROUP, block)

    def begin_right(p):
        turned = jnp.concatenate(
            [whole_ref[p, pl.ds(k, GROUP, stride=cols), :].astype(BF16) for k in range(cols)], axis=0
        )
        near_right[p] = project(right_rows[...], turned).reshape(chips, layers, GROUP * cols)
        mine = c * layers + pair
        for hop in hops:
            to = chip_at(*hop)
            send(
                near_right.at[p, to], met_right.at[p, mine], near_right_sems, p,
                core_at(to, z, side),
            )

        @pl.when(c == side)
        def _():
            met_right[p, mine] = near_right[p, a]

        @pl.when(c != side)
        def _():
            send(
                near_right.at[p, a], met_right.at[p, mine], near_right_sems, p,
                core_at(a, z, other),
            )

    def pass_right(p):
        settle_some(met_right, near_right_sems, 1, p)
        tiles = GROUP * cols // LANES

        def body(core, carry):
            for h in range(tiles):
                lanes = slice(h * LANES, (h + 1) * LANES)
                lines = turn_lanes([
                    met_right[p, core * layers + n, :, lanes].astype(F32) for n in range(layers)
                ])
                for n in range(layers):
                    at = (h * layers + n) * layers
                    turn_ref[at : at + layers, :] = lines[n]
            for h in range(parts):
                for n in range(layers):
                    line = turn_ref[pl.ds(h * GROUP * layers + n, GROUP, stride=layers), :]
                    far_right[p, n, core, h * GROUP : (h + 1) * GROUP, :] = line.astype(BF16)
            return carry

        with scope("rturn"):
            lax.fori_loop(0, CORES, body, 0)
        send_far(far_right, right_lines, right_sems, p, c)

    def give_left(p):
        settle(got_left.at[p, pl.ds(0, layers - 1)], far_left_sems, 1, p)

        def body(h, carry):
            for e in range(halves):
                lanes = pl.ds(pl.multiple_of((h * halves + e) * LANES, LANES), LANES)
                lines = turn_lanes([got_left[p, n, :, lanes].astype(F32) for n in range(layers)])
                for n in range(layers):
                    at = (e * layers + n) * GROUP
                    turn_ref[at : at + GROUP, :] = lines[n]
            lanes = pl.ds(pl.multiple_of(h * LANES, LANES), LANES)
            for d in range(GROUP):
                line = turn_ref[pl.ds(d, GROUP, stride=GROUP), :]
                near_left[p, d, :, lanes] = line.astype(BF16)
            return carry

        with scope("lturn"):
            lax.fori_loop(0, parts, body, 0)
        mine = c * chips + a
        for hop in hops:
            to = chip_at(*hop)
            for core in (c, other):
                send(
                    near_left.at[p, to], left_lines.at[p, mine], left_sems, p,
                    core_at(to, z, core),
                )
        send(near_left.at[p, a], left_lines.at[p, mine], left_sems, p, core_at(a, z, other))
        left_lines[p, mine] = near_left[p, a]

    deep = near_left.shape[-1]

    def meet(q, p):
        if p == 0:
            settle(left_lines.at[q, pl.ds(0, CORES * chips - 1)], left_sems, 1, q)
        if q == 0:
            settle(right_lines.at[p, pl.ds(0, layers - 1)], right_sems, 1, p)
        at = p * parts + q
        with scope("meet"):
            total = None
            for core in range(CORES):
                left = left_lines[q, core * chips : (core + 1) * chips].reshape(block, deep)
                right = jnp.concatenate(
                    [
                        right_lines[p, :, core, h * GROUP : (h + 1) * GROUP, :].reshape(LANES, LANES)
                        for h in range(parts)
                    ],
                    axis=0,
                )
                term = jnp.dot(left, right, preferred_element_type=F32)
                total = term if total is None else total + term
            mixed = (total * count ** (-0.5)).astype(BF16)
            mix_send[at] = mixed.reshape(chips, GROUP, LANES)
        for hop in hops:
            to = chip_at(*hop)
            send(mix_send.at[at, to], mix_recv.at[at, a], mix_sems, at, core_at(to, z, c))
        mix_recv[at, a] = mix_send[at, a]

    def give_back(q, p):
        at = p * parts + q
        settle(mix_recv.at[at, pl.ds(0, chips - 1)], mix_sems, 1, at)
        with scope("back"):
            for d in range(GROUP):
                turn_ref[d * GROUP : (d + 1) * GROUP, :] = mix_recv[at, d].astype(F32)
            for e in range(halves):
                lines = turn_lanes([
                    turn_ref[pl.ds(e * layers + n, GROUP, stride=GROUP), :] for n in range(layers)
                ])
                for n in range(layers):
                    back_send[at, n, :, e * LANES : (e + 1) * LANES] = lines[n].astype(BF16)
        send_far(back_send, back_recv, back_sems, at, c)

    def finish(q, p):
        at = p * parts + q
        settle(back_recv.at[at, pl.ds(0, layers - 1)], back_sems, 1, at)
        with scope("finish"):
            mixed = back_recv[at].reshape(width, block).astype(F32)
            centred = mixed - jnp.mean(mixed, axis=0, keepdims=True)
            scaled = centred * lax.rsqrt(jnp.mean(centred * centred, axis=0, keepdims=True) + 1e-05)
            scaled = jnp.concatenate(
                [scaled[:, e * LANES : (e + 1) * LANES] * mid_wide[...] for e in range(halves)], axis=1
            ).astype(BF16)
            result = lax.dot_general(
                scaled, out_weight[...], (((0,), (0,)), ((), ())), preferred_element_type=F32
            )
            result = (result * gate_ref[p, q * block : (q + 1) * block, :]).astype(BF16)
            out_ref[q * GROUP : (q + 1) * GROUP, p * GROUP : (p + 1) * GROUP, :] = result.reshape(
                GROUP, GROUP, width
            )

    for p in range(parts):
        begin(p)
        if p == 0:
            with scope("bar"):
                pl.semaphore_wait(barrier, len(peers))
        send_far(far_left, got_left, far_left_sems, p, c)
        begin_right(p)

    with scope("gate"):
        fetches[parts + 3].wait()
        for h in range(parts):
            gate_ref[h] = jax.nn.sigmoid(
                jnp.dot(ready_ref[h], out_gate[...], preferred_element_type=F32)
            )
        fetches[parts + 4].wait()
        mid_wide[...] = jnp.broadcast_to(mid_gain[...].reshape(1, width), (width, width)).T
        fetches[parts + 5].wait()

    pass_right(0)
    give_left(0)
    for p in range(1, parts):
        pass_right(p)
    for q in range(1, parts):
        give_left(q)
    last = parts - 1
    for p in range(parts):
        for q in range(parts):
            meet(q, p)
        if p > 0:
            for q in range(parts):
                give_back(q, p - 1)
                if p > 1:
                    finish(q, p - 2)
    for q in range(parts):
        give_back(q, last)
    for p in range(max(last - 1, 0), parts):
        for q in range(parts):
            finish(q, p)

    for p in range(parts):
        settle(far_left.at[p, pl.ds(0, layers - 1)], far_left_sems, 0, p)
        settle(left_lines.at[p, pl.ds(0, CORES * chips - 1)], left_sems, 0, p)
        settle_some(met_right, near_right_sems, 0, p)
        settle(far_right.at[p, pl.ds(0, layers - 1)], right_sems, 0, p)
    for at in range(parts * parts):
        settle(mix_send.at[at, pl.ds(0, chips - 1)], mix_sems, 0, at)
        settle(back_send.at[at, pl.ds(0, layers - 1)], back_sems, 0, at)


def by_kernel(pair_state, in_gain, left_weight, right_weight, mid_gain, out_weight, out_gate):
    rows, cols, width = pair_state.shape
    chips = lax.axis_size("first")
    layers = lax.axis_size("second") // CORES
    count = cols * lax.axis_size("second")
    parts = rows // GROUP
    block = GROUP * GROUP
    lanes = parts * block
    deep = parts * LANES
    changed = pl.pallas_call(
        functools.partial(triangle_kernel, layers, chips, count),
        out_shape=jax.ShapeDtypeStruct((rows, cols, width), BF16),
        in_specs=[pl.BlockSpec(memory_space=pltpu.MemorySpace.HBM)] * 7,
        out_specs=pl.BlockSpec(memory_space=pltpu.VMEM),
        scratch_shapes=[
            pltpu.VMEM((rows, cols, width), BF16),
            pltpu.VMEM((width,), F32),
            pltpu.VMEM(left_weight.shape, BF16),
            pltpu.VMEM(right_weight.shape, BF16),
            pltpu.VMEM((width,), F32),
            pltpu.VMEM(out_weight.shape, BF16),
            pltpu.VMEM(out_gate.shape, BF16),
            pltpu.SemaphoreType.DMA((parts + 6,)),
            pltpu.VMEM((width, width), BF16),
            pltpu.VMEM((width, width), BF16),
            pltpu.VMEM((width, width), F32),
            pltpu.VMEM((parts, GROUP * cols, width), F32),
            pltpu.VMEM((parts, rows * GROUP, width), BF16),
            pltpu.VMEM((parts, rows * GROUP, width), F32),
            pltpu.VMEM((cols * layers, LANES), F32),
            pltpu.VMEM((parts, layers, GROUP, lanes), BF16),
            pltpu.VMEM((parts, layers, GROUP, lanes), BF16),
            pltpu.VMEM((parts, chips, GROUP, deep), BF16),
            pltpu.VMEM((parts, CORES * chips, GROUP, deep), BF16),
            pltpu.VMEM((parts, chips, layers, lanes), BF16),
            pltpu.VMEM((parts, CORES * layers, layers, lanes), BF16),
            pltpu.VMEM((parts, layers, CORES, cols, LANES), BF16),
            pltpu.VMEM((parts, layers, CORES, cols, LANES), BF16),
            pltpu.VMEM((parts * parts, chips, GROUP, LANES), BF16),
            pltpu.VMEM((parts * parts, chips, GROUP, LANES), BF16),
            pltpu.VMEM((parts * parts, layers, GROUP, block), BF16),
            pltpu.VMEM((parts * parts, layers, GROUP, block), BF16),
            pltpu.SemaphoreType.DMA((2, parts)),
            pltpu.SemaphoreType.DMA((2, parts)),
            pltpu.SemaphoreType.DMA((2, parts)),
            pltpu.SemaphoreType.DMA((2, parts)),
            pltpu.SemaphoreType.DMA((2, parts * parts)),
            pltpu.SemaphoreType.DMA((2, parts * parts)),
        ],
        compiler_params=pltpu.CompilerParams(
            collective_id=0, has_side_effects=True, vmem_limit_bytes=32 * 1024 * 1024
        ),
    )(
        *(
            pltpu.with_memory_space_constraint(value, pltpu.MemorySpace.HBM)
            for value in (
                pair_state, in_gain, left_weight, right_weight, mid_gain, out_weight, out_gate,
            )
        )
    )
    return changed


def unit_channels(values, channel_gain):
    centred = values - jnp.mean(values, axis=-1, keepdims=True)
    return (
        centred
        * lax.rsqrt(jnp.mean(centred * centred, axis=-1, keepdims=True) + 1e-05)
        * channel_gain
    )


def make_factors(pair_in, in_gain, left_weight, right_weight):
    ready = unit_channels(pair_in.astype(jnp.float32), in_gain).astype(jnp.bfloat16)
    ready = lax.optimization_barrier(ready)
    left = jnp.einsum("ijc,cd->ijd", ready, left_weight, preferred_element_type=jnp.float32)
    right = jnp.einsum("ijc,cd->ijd", ready, right_weight, preferred_element_type=jnp.float32)
    return (ready, left.astype(jnp.bfloat16), right.astype(jnp.bfloat16))


def finish_pair(mixed, ready, mid_gain, out_weight, out_gate):
    scaled = unit_channels(mixed.astype(jnp.float32), mid_gain).astype(jnp.bfloat16)
    scaled = lax.optimization_barrier(scaled)
    gate = jax.nn.sigmoid(
        jnp.einsum("ijc,cd->ijd", ready, out_gate, preferred_element_type=jnp.float32)
    )
    return (
        jnp.einsum("ijd,dc->ijc", scaled, out_weight, preferred_element_type=jnp.float32) * gate
    ).astype(jnp.bfloat16)


def by_collectives(pair_state, in_gain, left_weight, right_weight, mid_gain, out_weight, out_gate):
    ready, left, right = make_factors(pair_state, in_gain, left_weight, right_weight)
    count = pair_state.shape[1] * lax.axis_size("second")
    left_lines, right_lines = (
        lax.all_to_all(left, "second", split_axis=2, concat_axis=1, tiled=True),
        lax.all_to_all(right, "second", split_axis=2, concat_axis=1, tiled=True),
    )

    def meet(piece):
        return jnp.einsum("ikd,jkd->ijd", left_lines, piece, preferred_element_type=jnp.float32)

    strip = meet(lax.all_gather(right_lines, "first", axis=0, tiled=True))
    strip = (strip * count ** (-0.5)).astype(jnp.bfloat16)
    mixed = lax.all_to_all(strip, "second", split_axis=1, concat_axis=2, tiled=True)
    return finish_pair(mixed, ready, mid_gain, out_weight, out_gate)


def per_device(pair_state, *rest):
    groups, parts = lax.axis_size("first"), lax.axis_size("second")
    rows, cols, width = pair_state.shape
    left_out = rest[1].shape[1]
    fits = (
        groups == SIDE * SIDE
        and parts == CORES * 8
        and width == GROUP * 8
        and rows == cols
        and rows % GROUP == 0
        and left_out == width
    )
    return (by_kernel if fits else by_collectives)(pair_state, *rest)


def solution(mesh):
    in_specs = (P("first", "second", None), P(), P(), P(), P(), P(), P())
    out_specs = P("first", "second", None)
    return jax.shard_map(
        per_device, mesh=mesh, in_specs=in_specs, out_specs=out_specs, check_vma=False
    )
```

time: 61.6 us -> 54.7 us (0.89)
  Pallas kernels: 59.3 us -> 53.8 us
  local copies, waits for them, and re-layouts: 2.21 us -> 0.82 us
    pallas_call x1, Pallas kernels: 59.3 us -> 53.8 us  [by_kernel(): pl.pallas_call(functools.partial(triangle_kernel, layers, chips, count),...]
    reshape x1 -> x0, local copies, waits for them, and re-layouts: 0.74 us -> none  [by_kernel(): mid_gain.reshape(width, 1)]
    unnamed x3 -> x1, local copies, waits for them, and re-layouts: 1.47 us -> 0.82 us
where the time goes in v3:
time: 54.7 us; the launch traced here: 54.6 us
  Pallas kernels  53.8 us (98%)
  local copies, waits for them, and re-layouts  0.82 us (1%)
    pallas_call x1, Pallas kernels, by_kernel(): pl.pallas_call(functools.partial(triangle_kernel, layers, chips, count),...  53.8 us

profile of v3, /device:TPU:1, one launch (start us, length us, event | category | flops | bytes accessed | tf_op | source)
XLA Modules:
  0.0 54.6 jit_solution(4568298502816600615)
XLA Ops:
  0.0 53.8 %shard_map.73 = bf16[48,48,128]{2,1,0:T(8,128)(2,1)S(1)} custom-call(bf16[48,48,128]{2,1,0:T(8,128)(2,1)} %x_hbm.1, f32[128]{0:T(128)} %in_gain_hbm.1, bf16[128,128]{1,0:T(8,128)(2,1)} %left_weight_hbm.1, bf16[128,128]{1,0:T(8,128)(2,1)} %right_weight_hbm.1, f32[128]{0:T(128)} %mid_gain_hbm.1, bf16[128,128]{1,0:T(8,128)(2,1)} %out_weight_hbm.1, ...), custom_call_target="tpu_custom_call" | custom-call | tf_op jit(solution)/shard_map/pallas_call | solution.py:351
  53.8 0.8 %copy.9 = bf16[48,48,128]{2,1,0:T(8,128)(2,1)} copy(bf16[48,48,128]{2,1,0:T(8,128)(2,1)S(1)} %shard_map.73) | data formatting | bytes 1179648

commit v4 on v3

--- a/solution.py
+++ b/solution.py
@@ -16,6 +16,11 @@
 SIDE = 4
 LANES = 128
 GROUP = 16
+UNIT = 8
+PLAN = (
+    "a0 r0 a1 r1 a2 r2 f0 a3 f1 a4 f2 a5 f3 f4 m00 f5 m10 m20 m01 m11 m21 c00 c10 c20 "
+    "m02 m12 m22 c01 c11 c21 d00 d10 c02 c12 c22 d20 d01 d11 d21 d02 d12 d22"
+)
 
 
 def unit_rows(values, channel_gain):
@@ -53,12 +58,13 @@
     far_left, got_left, near_left, left_lines,
     near_right, met_right, far_right, right_lines,
     mix_send, mix_recv, back_send, back_recv,
-    far_left_sems, left_sems, near_right_sems, right_sems, mix_sems, back_sems,
+    far_left_sems, left_sems, pass_sems, near_right_sems, right_sems, mix_sems, back_sems,
 ):
     scope = jax.named_scope
     rows, cols, width = x_ref.shape
     parts = rows // GROUP
-    halves = GROUP // layers
+    units = rows // UNIT
+    halves = GROUP // UNIT
     block = GROUP * GROUP
     a = lax.axis_index("first")
     b = lax.axis_index("second")
@@ -150,9 +156,11 @@
         for h in range(parts):
             piece = ready[:, h].reshape(block, width)
             ready_ref[h, p * block : (p + 1) * block, :] = piece
-            far_left[p, :, :, h * block : (h + 1) * block] = project(
-                left_rows[...], piece
-            ).reshape(layers, GROUP, block)
+            made = project(left_rows[...], piece)
+            for e in range(halves):
+                far_left[p * halves + e, :, :, h * LANES : (h + 1) * LANES] = made[
+                    :, e * LANES : (e + 1) * LANES
+                ].reshape(layers, GROUP, LANES)
 
     def begin_right(p):
         turned = jnp.concatenate(
@@ -201,47 +209,49 @@
             lax.fori_loop(0, CORES, body, 0)
         send_far(far_right, right_lines, right_sems, p, c)
 
-    def give_left(p):
-        settle(got_left.at[p, pl.ds(0, layers - 1)], far_left_sems, 1, p)
-
-        def body(h, carry):
-            for e in range(halves):
-                lanes = pl.ds(pl.multiple_of((h * halves + e) * LANES, LANES), LANES)
-                lines = turn_lanes([got_left[p, n, :, lanes].astype(F32) for n in range(layers)])
-                for n in range(layers):
-                    at = (e * layers + n) * GROUP
+    def give_left(u):
+        settle(got_left.at[u, pl.ds(0, layers - 1)], far_left_sems, 1, u)
+        with scope("lturn"):
+            for h in range(parts):
+                lanes = slice(h * LANES, (h + 1) * LANES)
+                lines = turn_lanes([got_left[u, n, :, lanes].astype(F32) for n in range(layers)])
+                for n in range(UNIT):
+                    at = (h * UNIT + n) * GROUP
                     turn_ref[at : at + GROUP, :] = lines[n]
-            lanes = pl.ds(pl.multiple_of(h * LANES, LANES), LANES)
-            for d in range(GROUP):
-                line = turn_ref[pl.ds(d, GROUP, stride=GROUP), :]
-                near_left[p, d, :, lanes] = line.astype(BF16)
-            return carry
-
-        with scope("lturn"):
-            lax.fori_loop(0, parts, body, 0)
+                for d in range(GROUP):
+                    line = turn_ref[pl.ds(h * UNIT * GROUP + d, UNIT, stride=GROUP), :]
+                    near_left[u, d, :, lanes] = line.astype(BF16)
         mine = c * chips + a
         for hop in hops:
             to = chip_at(*hop)
-            for core in (c, other):
-                send(
-                    near_left.at[p, to], left_lines.at[p, mine], left_sems, p,
-                    core_at(to, z, core),
-                )
-        send(near_left.at[p, a], left_lines.at[p, mine], left_sems, p, core_at(a, z, other))
-        left_lines[p, mine] = near_left[p, a]
+            send(
+                near_left.at[u, to], left_lines.at[u, mine], left_sems, u, core_at(to, z, c)
+            )
+        left_lines[u, mine] = near_left[u, a]
+
+    def pass_left(u):
+        settle(left_lines.at[u, pl.ds(0, chips - 1)], left_sems, 1, u)
+        with scope("pass"):
+            own = pl.ds(c * chips, chips)
+            send(
+                left_lines.at[u, own], left_lines.at[u, own], pass_sems, u, core_at(a, z, other)
+            )
 
     deep = near_left.shape[-1]
 
     def meet(q, p):
         if p == 0:
-            settle(left_lines.at[q, pl.ds(0, CORES * chips - 1)], left_sems, 1, q)
+            for u in range(q * halves, (q + 1) * halves):
+                settle(left_lines.at[u, pl.ds(0, chips)], pass_sems, 1, u)
         if q == 0:
             settle(right_lines.at[p, pl.ds(0, layers - 1)], right_sems, 1, p)
         at = p * parts + q
         with scope("meet"):
             total = None
             for core in range(CORES):
-                left = left_lines[q, core * chips : (core + 1) * chips].reshape(block, deep)
+                left = left_lines[
+                    q * halves : (q + 1) * halves, core * chips : (core + 1) * chips
+                ].reshape(block, deep)
                 right = jnp.concatenate(
                     [
                         right_lines[p, :, core, h * GROUP : (h + 1) * GROUP, :].reshape(LANES, LANES)
@@ -252,7 +262,10 @@
                 term = jnp.dot(left, right, preferred_element_type=F32)
                 total = term if total is None else total + term
             mixed = (total * count ** (-0.5)).astype(BF16)
-            mix_send[at] = mixed.reshape(chips, GROUP, LANES)
+            for e in range(halves):
+                mix_send[at, :, e * UNIT : (e + 1) * UNIT, :] = mixed[
+                    e * LANES : (e + 1) * LANES
+                ].reshape(chips, UNIT, LANES)
         for hop in hops:
             to = chip_at(*hop)
             send(mix_send.at[at, to], mix_recv.at[at, a], mix_sems, at, core_at(to, z, c))
@@ -295,7 +308,8 @@
         if p == 0:
             with scope("bar"):
                 pl.semaphore_wait(barrier, len(peers))
-        send_far(far_left, got_left, far_left_sems, p, c)
+        for e in range(halves):
+            send_far(far_left, got_left, far_left_sems, p * halves + e, c)
         begin_right(p)
 
     with scope("gate"):
@@ -308,32 +322,20 @@
         mid_wide[...] = jnp.broadcast_to(mid_gain[...].reshape(1, width), (width, width)).T
         fetches[parts + 5].wait()
 
-    pass_right(0)
-    give_left(0)
-    for p in range(1, parts):
-        pass_right(p)
-    for q in range(1, parts):
-        give_left(q)
-    last = parts - 1
+    for step in PLAN.split():
+        name, *at = step
+        todo = {
+            "a": give_left, "r": pass_right, "f": pass_left, "m": meet, "c": give_back, "d": finish,
+        }[name]
+        todo(*(int(n) for n in at))
+
     for p in range(parts):
-        for q in range(parts):
-            meet(q, p)
-        if p > 0:
-            for q in range(parts):
-                give_back(q, p - 1)
-                if p > 1:
-                    finish(q, p - 2)
-    for q in range(parts):
-        give_back(q, last)
-    for p in range(max(last - 1, 0), parts):
-        for q in range(parts):
-            finish(q, p)
-
-    for p in range(parts):
-        settle(far_left.at[p, pl.ds(0, layers - 1)], far_left_sems, 0, p)
-        settle(left_lines.at[p, pl.ds(0, CORES * chips - 1)], left_sems, 0, p)
         settle_some(met_right, near_right_sems, 0, p)
         settle(far_right.at[p, pl.ds(0, layers - 1)], right_sems, 0, p)
+    for u in range(units):
+        settle(far_left.at[u, pl.ds(0, layers - 1)], far_left_sems, 0, u)
+        settle(near_left.at[u, pl.ds(0, chips - 1)], left_sems, 0, u)
+        settle(left_lines.at[u, pl.ds(0, chips)], pass_sems, 0, u)
     for at in range(parts * parts):
         settle(mix_send.at[at, pl.ds(0, chips - 1)], mix_sems, 0, at)
         settle(back_send.at[at, pl.ds(0, layers - 1)], back_sems, 0, at)
@@ -345,6 +347,7 @@
     layers = lax.axis_size("second") // CORES
     count = cols * lax.axis_size("second")
     parts = rows // GROUP
+    units = rows // UNIT
     block = GROUP * GROUP
     lanes = parts * block
     deep = parts * LANES
@@ -369,10 +372,10 @@
             pltpu.VMEM((parts, rows * GROUP, width), BF16),
             pltpu.VMEM((parts, rows * GROUP, width), F32),
             pltpu.VMEM((cols * layers, LANES), F32),
-            pltpu.VMEM((parts, layers, GROUP, lanes), BF16),
-            pltpu.VMEM((parts, layers, GROUP, lanes), BF16),
-            pltpu.VMEM((parts, chips, GROUP, deep), BF16),
-            pltpu.VMEM((parts, CORES * chips, GROUP, deep), BF16),
+            pltpu.VMEM((units, layers, GROUP, deep), BF16),
+            pltpu.VMEM((units, layers, GROUP, deep), BF16),
+            pltpu.VMEM((units, chips, UNIT, deep), BF16),
+            pltpu.VMEM((units, CORES * chips, UNIT, deep), BF16),
             pltpu.VMEM((parts, chips, layers, lanes), BF16),
             pltpu.VMEM((parts, CORES * layers, layers, lanes), BF16),
             pltpu.VMEM((parts, layers, CORES, cols, LANES), BF16),
@@ -381,8 +384,9 @@
             pltpu.VMEM((parts * parts, chips, GROUP, LANES), BF16),
             pltpu.VMEM((parts * parts, layers, GROUP, block), BF16),
             pltpu.VMEM((parts * parts, layers, GROUP, block), BF16),
-            pltpu.SemaphoreType.DMA((2, parts)),
-            pltpu.SemaphoreType.DMA((2, parts)),
+            pltpu.SemaphoreType.DMA((2, units)),
+            pltpu.SemaphoreType.DMA((2, units)),
+            pltpu.SemaphoreType.DMA((2, units)),
             pltpu.SemaphoreType.DMA((2, parts)),
             pltpu.SemaphoreType.DMA((2, parts)),
             pltpu.SemaphoreType.DMA((2, parts * parts)),

time: 54.7 us -> 52.8 us (0.965)
  Pallas kernels: 53.8 us -> 51.9 us
    pallas_call x1, Pallas kernels: 53.8 us -> 51.9 us  [by_kernel(): pl.pallas_call(functools.partial(triangle_kernel, layers, chips, count),...]
where the time goes in v4:
time: 52.8 us; the launch traced here: 52.7 us
  Pallas kernels  51.9 us (98%)
  local copies, waits for them, and re-layouts  0.82 us (2%)
    pallas_call x1, Pallas kernels, by_kernel(): pl.pallas_call(functools.partial(triangle_kernel, layers, chips, count),...  51.9 us

profile of v4, /device:TPU:1, one launch (start us, length us, event | category | flops | bytes accessed | tf_op | source)
XLA Modules:
  0.0 52.7 jit_solution(2111737681800439710)
XLA Ops:
  0.0 51.9 %shard_map.73 = bf16[48,48,128]{2,1,0:T(8,128)(2,1)S(1)} custom-call(bf16[48,48,128]{2,1,0:T(8,128)(2,1)} %x_hbm.1, f32[128]{0:T(128)} %in_gain_hbm.1, bf16[128,128]{1,0:T(8,128)(2,1)} %left_weight_hbm.1, bf16[128,128]{1,0:T(8,128)(2,1)} %right_weight_hbm.1, f32[128]{0:T(128)} %mid_gain_hbm.1, bf16[128,128]{1,0:T(8,128)(2,1)} %out_weight_hbm.1, ...), custom_call_target="tpu_custom_call" | custom-call | tf_op jit(solution)/shard_map/pallas_call | solution.py:354
  51.9 0.8 %copy.9 = bf16[48,48,128]{2,1,0:T(8,128)(2,1)} copy(bf16[48,48,128]{2,1,0:T(8,128)(2,1)S(1)} %shard_map.73) | data formatting | bytes 1179648

commit v5 on v4

--- a/solution.py
+++ b/solution.py
@@ -18,8 +18,11 @@
 GROUP = 16
 UNIT = 8
 PLAN = (
-    "a0 r0 a1 r1 a2 r2 f0 a3 f1 a4 f2 a5 f3 f4 m00 f5 m10 m20 m01 m11 m21 c00 c10 c20 "
-    "m02 m12 m22 c01 c11 c21 d00 d10 c02 c12 c22 d20 d01 d11 d21 d02 d12 d22"
+    "a0", "r0", "a1", "r1", "a2", "r2", "f0", "a3", "f1", "a4", "f2", "a5", "f3", "f4",
+    "m00", "f5", "m10", "m20", "m01", "m11", "m21", "c00", "c10", "h00", "c20", "h10",
+    "m02", "m12", "m22", "c01", "h20", "c11", "c21", "h01", "d00", "d10", "c02", "c12",
+    "c22", "h11", "h21", "h02", "h12", "h22", "d20", "d01", "d11", "d21", "d02", "d12",
+    "d22",
 )
 
 
@@ -271,6 +274,13 @@
             send(mix_send.at[at, to], mix_recv.at[at, a], mix_sems, at, core_at(to, z, c))
         mix_recv[at, a] = mix_send[at, a]
 
+    def send_back(at, order):
+        for n in order:
+            to = n + (n + layers - z) // layers
+            send(
+                back_send.at[at, to], back_recv.at[at, z], back_sems, at, core_at(a, to, c)
+            )
+
     def give_back(q, p):
         at = p * parts + q
         settle(mix_recv.at[at, pl.ds(0, chips - 1)], mix_sems, 1, at)
@@ -283,7 +293,11 @@
                 ])
                 for n in range(layers):
                     back_send[at, n, :, e * LANES : (e + 1) * LANES] = lines[n].astype(BF16)
-        send_far(back_send, back_recv, back_sems, at, c)
+        send_back(at, range(layers // 2))
+        back_recv[at, z] = back_send[at, z]
+
+    def give_high(q, p):
+        send_back(p * parts + q, range(layers // 2, layers - 1))
 
     def finish(q, p):
         at = p * parts + q
@@ -322,10 +336,11 @@
         mid_wide[...] = jnp.broadcast_to(mid_gain[...].reshape(1, width), (width, width)).T
         fetches[parts + 5].wait()
 
-    for step in PLAN.split():
+    for step in PLAN:
         name, *at = step
         todo = {
-            "a": give_left, "r": pass_right, "f": pass_left, "m": meet, "c": give_back, "d": finish,
+            "a": give_left, "r": pass_right, "f": pass_left, "m": meet, "c": give_back, "h": give_high,
+            "d": finish,
         }[name]
         todo(*(int(n) for n in at))
 

time: 52.8 us -> 52.8 us (level)
  no operation moved by 1% of the time
where the time goes in v5:
time: 52.8 us; the launch traced here: 52.7 us
  Pallas kernels  51.9 us (98%)
  local copies, waits for them, and re-layouts  0.82 us (2%)
    pallas_call x1, Pallas kernels, by_kernel(): pl.pallas_call(functools.partial(triangle_kernel, layers, chips, count),...  51.9 us

profile of v5, /device:TPU:1, one launch (start us, length us, event | category | flops | bytes accessed | tf_op | source)
XLA Modules:
  0.0 52.7 jit_solution(3350178859451753937)
XLA Ops:
  0.0 51.9 %shard_map.73 = bf16[48,48,128]{2,1,0:T(8,128)(2,1)S(1)} custom-call(bf16[48,48,128]{2,1,0:T(8,128)(2,1)} %x_hbm.1, f32[128]{0:T(128)} %in_gain_hbm.1, bf16[128,128]{1,0:T(8,128)(2,1)} %left_weight_hbm.1, bf16[128,128]{1,0:T(8,128)(2,1)} %right_weight_hbm.1, f32[128]{0:T(128)} %mid_gain_hbm.1, bf16[128,128]{1,0:T(8,128)(2,1)} %out_weight_hbm.1, ...), custom_call_target="tpu_custom_call" | custom-call | tf_op jit(solution)/shard_map/pallas_call | solution.py:369
  51.9 0.8 %copy.9 = bf16[48,48,128]{2,1,0:T(8,128)(2,1)} copy(bf16[48,48,128]{2,1,0:T(8,128)(2,1)S(1)} %shard_map.73) | data formatting | bytes 1179648

commit v6 on v4

--- a/solution.py
+++ b/solution.py
@@ -17,9 +17,13 @@
 LANES = 128
 GROUP = 16
 UNIT = 8
+LEFTS = ((0, 1), (1, 1), (2, 1), (3, 1), (4, 1), (5, 1))
+BLOCKS = ((0, 1), (1, 1), (2, 1), (3, 1), (4, 1), (5, 1), (6, 3))
 PLAN = (
-    "a0 r0 a1 r1 a2 r2 f0 a3 f1 a4 f2 a5 f3 f4 m00 f5 m10 m20 m01 m11 m21 c00 c10 c20 "
-    "m02 m12 m22 c01 c11 c21 d00 d10 c02 c12 c22 d20 d01 d11 d21 d02 d12 d22"
+    "a0", "r0", "a1", "r1", "a2", "r2", "f0", "a3", "f1", "a4", "f2", "a5", "f3", "f4",
+    "m0", "f5", "m1", "m2", "m3", "m4", "m5", "c0", "c1", "h0", "c2", "h1", "m6", "c3",
+    "h2", "c4", "c5", "h3", "d0", "d1", "h4", "c6", "h5", "h6", "d2", "d3", "d4", "d5",
+    "d6",
 )
 
 
@@ -119,28 +123,31 @@
 
     def send(src, dst, sems, at, peer):
         pltpu.make_async_remote_copy(
-            src_ref=src, dst_ref=dst, send_sem=sems.at[0, at], recv_sem=sems.at[1, at],
+            src_ref=src, dst_ref=dst, send_sem=sems.at[sems.shape[0] - 1], recv_sem=sems.at[at],
             device_id=peer, device_id_type=MESH,
         ).start()
 
-    def settle(like, sems, way, at):
+    def settle(like, sem):
         with scope("wait"):
-            pltpu.make_async_copy(like, like, sems.at[way, at]).wait()
-
-    def settle_some(like, sems, way, at):
+            pltpu.make_async_copy(like, like, sem).wait()
+
+    def settle_some(like, span, sem):
         @pl.when(c == side)
         def _():
-            settle(like.at[at, pl.ds(0, chips - 1)], sems, way, at)
+            settle(like.at[span, pl.ds(0, chips - 1)], sem)
 
         @pl.when(c != side)
         def _():
-            settle(like.at[at], sems, way, at)
-
-    def send_far(src, dst, sems, p, core):
+            settle(like.at[span], sem)
+
+    def sent(sems):
+        return sems.at[sems.shape[0] - 1]
+
+    def send_far(src, dst, sems, at, span):
         for s in steps:
             to = layer_at(s)
-            send(src.at[p, to], dst.at[p, z], sems, p, core_at(a, to, core))
-        dst[p, z] = src[p, z]
+            send(src.at[span, to], dst.at[span, z], sems, at, core_at(a, to, c))
+        dst[span, z] = src[span, z]
 
     def project(weight, lines):
         return lax.dot_general(
@@ -187,7 +194,7 @@
             )
 
     def pass_right(p):
-        settle_some(met_right, near_right_sems, 1, p)
+        settle_some(met_right, pl.ds(p, 1), near_right_sems.at[p])
         tiles = GROUP * cols // LANES
 
         def body(core, carry):
@@ -207,109 +214,145 @@
 
         with scope("rturn"):
             lax.fori_loop(0, CORES, body, 0)
-        send_far(far_right, right_lines, right_sems, p, c)
-
-    def give_left(u):
-        settle(got_left.at[u, pl.ds(0, layers - 1)], far_left_sems, 1, u)
+        send_far(far_right, right_lines, right_sems, p, pl.ds(p, 1))
+
+    def give_left(g):
+        first, size = LEFTS[g]
+        span = pl.ds(first, size)
+        settle(got_left.at[span, pl.ds(0, layers - 1)], far_left_sems.at[g])
         with scope("lturn"):
-            for h in range(parts):
-                lanes = slice(h * LANES, (h + 1) * LANES)
-                lines = turn_lanes([got_left[u, n, :, lanes].astype(F32) for n in range(layers)])
-                for n in range(UNIT):
-                    at = (h * UNIT + n) * GROUP
-                    turn_ref[at : at + GROUP, :] = lines[n]
-                for d in range(GROUP):
-                    line = turn_ref[pl.ds(h * UNIT * GROUP + d, UNIT, stride=GROUP), :]
-                    near_left[u, d, :, lanes] = line.astype(BF16)
+            for u in range(first, first + size):
+                for h in range(parts):
+                    lanes = slice(h * LANES, (h + 1) * LANES)
+                    lines = turn_lanes([
+                        got_left[u, n, :, lanes].astype(F32) for n in range(layers)
+                    ])
+                    for n in range(UNIT):
+                        at = (h * UNIT + n) * GROUP
+                        turn_ref[at : at + GROUP, :] = lines[n]
+                    for d in range(GROUP):
+                        line = turn_ref[pl.ds(h * UNIT * GROUP + d, UNIT, stride=GROUP), :]
+                        near_left[u, d, :, lanes] = line.astype(BF16)
         mine = c * chips + a
         for hop in hops:
             to = chip_at(*hop)
             send(
-                near_left.at[u, to], left_lines.at[u, mine], left_sems, u, core_at(to, z, c)
-            )
-        left_lines[u, mine] = near_left[u, a]
-
-    def pass_left(u):
-        settle(left_lines.at[u, pl.ds(0, chips - 1)], left_sems, 1, u)
+                near_left.at[span, to], left_lines.at[span, mine], left_sems, g,
+                core_at(to, z, c),
+            )
+        left_lines[span, mine] = near_left[span, a]
+
+    def pass_left(g):
+        first, size = LEFTS[g]
+        span = pl.ds(first, size)
+        settle(left_lines.at[span, pl.ds(0, chips - 1)], left_sems.at[g])
         with scope("pass"):
-            own = pl.ds(c * chips, chips)
-            send(
-                left_lines.at[u, own], left_lines.at[u, own], pass_sems, u, core_at(a, z, other)
-            )
+            own = left_lines.at[span, pl.ds(c * chips, chips)]
+            send(own, own, pass_sems, g, core_at(a, z, other))
 
     deep = near_left.shape[-1]
 
-    def meet(q, p):
-        if p == 0:
-            for u in range(q * halves, (q + 1) * halves):
-                settle(left_lines.at[u, pl.ds(0, chips)], pass_sems, 1, u)
-        if q == 0:
-            settle(right_lines.at[p, pl.ds(0, layers - 1)], right_sems, 1, p)
-        at = p * parts + q
-        with scope("meet"):
-            total = None
-            for core in range(CORES):
-                left = left_lines[
-                    q * halves : (q + 1) * halves, core * chips : (core + 1) * chips
-                ].reshape(block, deep)
-                right = jnp.concatenate(
-                    [
-                        right_lines[p, :, core, h * GROUP : (h + 1) * GROUP, :].reshape(LANES, LANES)
-                        for h in range(parts)
-                    ],
-                    axis=0,
-                )
-                term = jnp.dot(left, right, preferred_element_type=F32)
-                total = term if total is None else total + term
-            mixed = (total * count ** (-0.5)).astype(BF16)
-            for e in range(halves):
-                mix_send[at, :, e * UNIT : (e + 1) * UNIT, :] = mixed[
-                    e * LANES : (e + 1) * LANES
-                ].reshape(chips, UNIT, LANES)
+    met = set()
+
+    def meet(g):
+        first, size = BLOCKS[g]
+        span = pl.ds(first, size)
+        for at in range(first, first + size):
+            p, q = at // parts, at % parts
+            for n, (unit, many) in enumerate(LEFTS):
+                if unit < (q + 1) * halves and ("left", n) not in met:
+                    met.add(("left", n))
+                    settle(left_lines.at[pl.ds(unit, many), pl.ds(0, chips)], pass_sems.at[n])
+            if ("right", p) not in met:
+                met.add(("right", p))
+                settle(right_lines.at[p, pl.ds(0, layers - 1)], right_sems.at[p])
+            with scope("meet"):
+                total = None
+                for core in range(CORES):
+                    left = left_lines[
+                        q * halves : (q + 1) * halves, core * chips : (core + 1) * chips
+                    ].reshape(block, deep)
+                    right = jnp.concatenate(
+                        [
+                            right_lines[p, :, core, h * GROUP : (h + 1) * GROUP, :].reshape(LANES, LANES)
+                            for h in range(parts)
+                        ],
+                        axis=0,
+                    )
+                    term = jnp.dot(left, right, preferred_element_type=F32)
+                    total = term if total is None else total + term
+                mixed = (total * count ** (-0.5)).astype(BF16)
+                for e in range(halves):
+                    mix_send[at, :, e * UNIT : (e + 1) * UNIT, :] = mixed[
+                        e * LANES : (e + 1) * LANES
+                    ].reshape(chips, UNIT, LANES)
         for hop in hops:
             to = chip_at(*hop)
-            send(mix_send.at[at, to], mix_recv.at[at, a], mix_sems, at, core_at(to, z, c))
-        mix_recv[at, a] = mix_send[at, a]
-
-    def give_back(q, p):
-        at = p * parts + q
-        settle(mix_recv.at[at, pl.ds(0, chips - 1)], mix_sems, 1, at)
+            send(
+                mix_send.at[span, to], mix_recv.at[span, a], mix_sems, g, core_at(to, z, c)
+            )
+        mix_recv[span, a] = mix_send[span, a]
+
+    def send_back(g, order):
+        span = pl.ds(*BLOCKS[g])
+        for n in order:
+            to = n + (n + layers - z) // layers
+            send(
+                back_send.at[span, to], back_recv.at[span, z], back_sems, g, core_at(a, to, c)
+            )
+
+    def give_back(g):
+        first, size = BLOCKS[g]
+        span = pl.ds(first, size)
+        settle(mix_recv.at[span, pl.ds(0, chips - 1)], mix_sems.at[g])
         with scope("back"):
-            for d in range(GROUP):
-                turn_ref[d * GROUP : (d + 1) * GROUP, :] = mix_recv[at, d].astype(F32)
-            for e in range(halves):
-                lines = turn_lanes([
-                    turn_ref[pl.ds(e * layers + n, GROUP, stride=GROUP), :] for n in range(layers)
-                ])
-                for n in range(layers):
-                    back_send[at, n, :, e * LANES : (e + 1) * LANES] = lines[n].astype(BF16)
-        send_far(back_send, back_recv, back_sems, at, c)
-
-    def finish(q, p):
-        at = p * parts + q
-        settle(back_recv.at[at, pl.ds(0, layers - 1)], back_sems, 1, at)
+            for at in range(first, first + size):
+                for d in range(GROUP):
+                    turn_ref[d * GROUP : (d + 1) * GROUP, :] = mix_recv[at, d].astype(F32)
+                for e in range(halves):
+                    lines = turn_lanes([
+                        turn_ref[pl.ds(e * layers + n, GROUP, stride=GROUP), :]
+                        for n in range(layers)
+                    ])
+                    for n in range(layers):
+                        back_send[at, n, :, e * LANES : (e + 1) * LANES] = lines[n].astype(BF16)
+        send_back(g, range(layers // 2))
+        back_recv[span, z] = back_send[span, z]
+
+    def give_high(g):
+        send_back(g, range(layers // 2, layers - 1))
+
+    def finish(g):
+        first, size = BLOCKS[g]
+        settle(back_recv.at[pl.ds(first, size), pl.ds(0, layers - 1)], back_sems.at[g])
         with scope("finish"):
-            mixed = back_recv[at].reshape(width, block).astype(F32)
-            centred = mixed - jnp.mean(mixed, axis=0, keepdims=True)
-            scaled = centred * lax.rsqrt(jnp.mean(centred * centred, axis=0, keepdims=True) + 1e-05)
-            scaled = jnp.concatenate(
-                [scaled[:, e * LANES : (e + 1) * LANES] * mid_wide[...] for e in range(halves)], axis=1
-            ).astype(BF16)
-            result = lax.dot_general(
-                scaled, out_weight[...], (((0,), (0,)), ((), ())), preferred_element_type=F32
-            )
-            result = (result * gate_ref[p, q * block : (q + 1) * block, :]).astype(BF16)
-            out_ref[q * GROUP : (q + 1) * GROUP, p * GROUP : (p + 1) * GROUP, :] = result.reshape(
-                GROUP, GROUP, width
-            )
+            for at in range(first, first + size):
+                p, q = at // parts, at % parts
+                mixed = back_recv[at].reshape(width, block).astype(F32)
+                centred = mixed - jnp.mean(mixed, axis=0, keepdims=True)
+                scaled = centred * lax.rsqrt(
+                    jnp.mean(centred * centred, axis=0, keepdims=True) + 1e-05
+                )
+                scaled = jnp.concatenate(
+                    [scaled[:, e * LANES : (e + 1) * LANES] * mid_wide[...] for e in range(halves)],
+                    axis=1,
+                ).astype(BF16)
+                result = lax.dot_general(
+                    scaled, out_weight[...], (((0,), (0,)), ((), ())), preferred_element_type=F32
+                )
+                result = (result * gate_ref[p, q * block : (q + 1) * block, :]).astype(BF16)
+                out_ref[
+                    q * GROUP : (q + 1) * GROUP, p * GROUP : (p + 1) * GROUP, :
+                ] = result.reshape(GROUP, GROUP, width)
 
     for p in range(parts):
         begin(p)
         if p == 0:
             with scope("bar"):
                 pl.semaphore_wait(barrier, len(peers))
-        for e in range(halves):
-            send_far(far_left, got_left, far_left_sems, p * halves + e, c)
+        for g, (first, size) in enumerate(LEFTS):
+            if p * halves < first + size <= (p + 1) * halves:
+                send_far(far_left, got_left, far_left_sems, g, pl.ds(first, size))
         begin_right(p)
 
     with scope("gate"):
@@ -322,23 +365,21 @@
         mid_wide[...] = jnp.broadcast_to(mid_gain[...].reshape(1, width), (width, width)).T
         fetches[parts + 5].wait()
 
-    for step in PLAN.split():
-        name, *at = step
+    for step in PLAN:
         todo = {
-            "a": give_left, "r": pass_right, "f": pass_left, "m": meet, "c": give_back, "d": finish,
-        }[name]
-        todo(*(int(n) for n in at))
-
-    for p in range(parts):
-        settle_some(met_right, near_right_sems, 0, p)
-        settle(far_right.at[p, pl.ds(0, layers - 1)], right_sems, 0, p)
-    for u in range(units):
-        settle(far_left.at[u, pl.ds(0, layers - 1)], far_left_sems, 0, u)
-        settle(near_left.at[u, pl.ds(0, chips - 1)], left_sems, 0, u)
-        settle(left_lines.at[u, pl.ds(0, chips)], pass_sems, 0, u)
-    for at in range(parts * parts):
-        settle(mix_send.at[at, pl.ds(0, chips - 1)], mix_sems, 0, at)
-        settle(back_send.at[at, pl.ds(0, layers - 1)], back_sems, 0, at)
+            "a": give_left, "r": pass_right, "f": pass_left, "m": meet, "c": give_back,
+            "h": give_high, "d": finish,
+        }[step[0]]
+        todo(int(step[1:]))
+
+    others = pl.ds(0, layers - 1)
+    settle(far_left.at[:, others], sent(far_left_sems))
+    settle(near_left.at[:, pl.ds(0, chips - 1)], sent(left_sems))
+    settle(left_lines.at[:, pl.ds(0, chips)], sent(pass_sems))
+    settle_some(met_right, pl.ds(0, parts), sent(near_right_sems))
+    settle(far_right.at[:, others], sent(right_sems))
+    settle(mix_send.at[:, pl.ds(0, chips - 1)], sent(mix_sems))
+    settle(back_send.at[:, others], sent(back_sems))
 
 
 def by_kernel(pair_state, in_gain, left_weight, right_weight, mid_gain, out_weight, out_gate):
@@ -384,13 +425,13 @@
             pltpu.VMEM((parts * parts, chips, GROUP, LANES), BF16),
             pltpu.VMEM((parts * parts, layers, GROUP, block), BF16),
             pltpu.VMEM((parts * parts, layers, GROUP, block), BF16),
-            pltpu.SemaphoreType.DMA((2, units)),
-            pltpu.SemaphoreType.DMA((2, units)),
-            pltpu.SemaphoreType.DMA((2, units)),
-            pltpu.SemaphoreType.DMA((2, parts)),
-            pltpu.SemaphoreType.DMA((2, parts)),
-            pltpu.SemaphoreType.DMA((2, parts * parts)),
-            pltpu.SemaphoreType.DMA((2, parts * parts)),
+            pltpu.SemaphoreType.DMA((len(LEFTS) + 1,)),
+            pltpu.SemaphoreType.DMA((len(LEFTS) + 1,)),
+            pltpu.SemaphoreType.DMA((len(LEFTS) + 1,)),
+            pltpu.SemaphoreType.DMA((parts + 1,)),
+            pltpu.SemaphoreType.DMA((parts + 1,)),
+            pltpu.SemaphoreType.DMA((len(BLOCKS) + 1,)),
+            pltpu.SemaphoreType.DMA((len(BLOCKS) + 1,)),
         ],
         compiler_params=pltpu.CompilerParams(
             collective_id=0, has_side_effects=True, vmem_limit_bytes=32 * 1024 * 1024
@@ -460,7 +501,7 @@
         and parts == CORES * 8
         and width == GROUP * 8
         and rows == cols
-        and rows % GROUP == 0
+        and rows == 3 * GROUP
         and left_out == width
     )
     return (by_kernel if fits else by_collectives)(pair_state, *rest)

time: 52.8 us -> 52.2 us (0.989)
  Pallas kernels: 51.9 us -> 51.3 us
    pallas_call x1, Pallas kernels: 51.9 us -> 51.3 us  [by_kernel(): pl.pallas_call(functools.partial(triangle_kernel, layers, chips, count),...]
where the time goes in v6:
time: 52.2 us; the launch traced here: 52.1 us
  Pallas kernels  51.3 us (98%)
  local copies, waits for them, and re-layouts  0.82 us (2%)
    pallas_call x1, Pallas kernels, by_kernel(): pl.pallas_call(functools.partial(triangle_kernel, layers, chips, count),...  51.3 us

profile of v6, /device:TPU:1, one launch (start us, length us, event | category | flops | bytes accessed | tf_op | source)
XLA Modules:
  0.0 52.1 jit_solution(650652725965985111)
XLA Ops:
  0.0 51.3 %shard_map.73 = bf16[48,48,128]{2,1,0:T(8,128)(2,1)S(1)} custom-call(bf16[48,48,128]{2,1,0:T(8,128)(2,1)} %x_hbm.1, f32[128]{0:T(128)} %in_gain_hbm.1, bf16[128,128]{1,0:T(8,128)(2,1)} %left_weight_hbm.1, bf16[128,128]{1,0:T(8,128)(2,1)} %right_weight_hbm.1, f32[128]{0:T(128)} %mid_gain_hbm.1, bf16[128,128]{1,0:T(8,128)(2,1)} %out_weight_hbm.1, ...), custom_call_target="tpu_custom_call" | custom-call | tf_op jit(solution)/shard_map/pallas_call | solution.py:395
  51.3 0.8 %copy.9 = bf16[48,48,128]{2,1,0:T(8,128)(2,1)} copy(bf16[48,48,128]{2,1,0:T(8,128)(2,1)S(1)} %shard_map.73) | data formatting | bytes 1179648

commit v7 on v6

--- a/solution.py
+++ b/solution.py
@@ -21,7 +21,7 @@
 BLOCKS = ((0, 1), (1, 1), (2, 1), (3, 1), (4, 1), (5, 1), (6, 3))
 PLAN = (
     "a0", "r0", "a1", "r1", "a2", "r2", "f0", "a3", "f1", "a4", "f2", "a5", "f3", "f4",
-    "m0", "f5", "m1", "m2", "m3", "m4", "m5", "c0", "c1", "h0", "c2", "h1", "m6", "c3",
+    "m0", "m1", "f5", "m2", "m3", "m4", "m5", "c0", "c1", "h0", "c2", "h1", "m6", "c3",
     "h2", "c4", "c5", "h3", "d0", "d1", "h4", "c6", "h5", "h6", "d2", "d3", "d4", "d5",
     "d6",
 )
@@ -91,10 +91,12 @@
     steps = [4, 3, 5, 2, 6, 1, 7]
 
     barrier = pltpu.get_barrier_semaphore()
-    peers = [core_at(a, z, other)]
-    peers += [core_at(a, layer_at(s), c) for s in steps]
-    for hop in hops:
-        peers += [core_at(chip_at(*hop), z, c), core_at(chip_at(*hop), z, other)]
+    peers = [(0, core_at(a, z, other))]
+    peers += [(min(s, layers - s), core_at(a, layer_at(s), c)) for s in steps]
+    for dy, dx in hops:
+        away = min(dy, SIDE - dy) + min(dx, SIDE - dx)
+        peers += [(away, core_at(chip_at(dy, dx), z, core)) for core in (other, c)]
+    peers = [peer for _, peer in sorted(peers, key=lambda pair: -pair[0])]
     for peer in peers:
         pl.semaphore_signal(barrier, inc=1, device_id=peer, device_id_type=MESH)
 

time: 52.2 us -> 51.7 us (level)
  the two profiles are of different devices: /device:TPU:1 before, /device:TPU:32 now
where the time goes in v7:
time: 51.7 us; the launch traced here: 51.6 us
  Pallas kernels  50.8 us (98%)
  local copies, waits for them, and re-layouts  0.82 us (2%)
    pallas_call x1, Pallas kernels, by_kernel(): pl.pallas_call(functools.partial(triangle_kernel, layers, chips, count),...  50.8 us

profile of v7, /device:TPU:32, one launch (start us, length us, event | category | flops | bytes accessed | tf_op | source)
XLA Modules:
  0.0 51.6 jit_solution(1202970675016191313)
XLA Ops:
  0.0 50.8 %shard_map.73 = bf16[48,48,128]{2,1,0:T(8,128)(2,1)S(1)} custom-call(bf16[48,48,128]{2,1,0:T(8,128)(2,1)} %x_hbm.1, f32[128]{0:T(128)} %in_gain_hbm.1, bf16[128,128]{1,0:T(8,128)(2,1)} %left_weight_hbm.1, bf16[128,128]{1,0:T(8,128)(2,1)} %right_weight_hbm.1, f32[128]{0:T(128)} %mid_gain_hbm.1, bf16[128,128]{1,0:T(8,128)(2,1)} %out_weight_hbm.1, ...), custom_call_target="tpu_custom_call" | custom-call | tf_op jit(solution)/shard_map/pallas_call | solution.py:397
  50.8 0.8 %copy.9 = bf16[48,48,128]{2,1,0:T(8,128)(2,1)} copy(bf16[48,48,128]{2,1,0:T(8,128)(2,1)S(1)} %shard_map.73) | data formatting | bytes 1179648

commit v8 on v7

--- a/solution.py
+++ b/solution.py
@@ -20,7 +20,7 @@
 LEFTS = ((0, 1), (1, 1), (2, 1), (3, 1), (4, 1), (5, 1))
 BLOCKS = ((0, 1), (1, 1), (2, 1), (3, 1), (4, 1), (5, 1), (6, 3))
 PLAN = (
-    "a0", "r0", "a1", "r1", "a2", "r2", "f0", "a3", "f1", "a4", "f2", "a5", "f3", "f4",
+    "a0", "a1", "r0", "r1", "a2", "r2", "a3", "f0", "f1", "a4", "f2", "a5", "f3", "f4",
     "m0", "m1", "f5", "m2", "m3", "m4", "m5", "c0", "c1", "h0", "c2", "h1", "m6", "c3",
     "h2", "c4", "c5", "h3", "d0", "d1", "h4", "c6", "h5", "h6", "d2", "d3", "d4", "d5",
     "d6",

time: 51.7 us -> 51.4 us (level)
  no operation moved by 1% of the time
where the time goes in v8:
time: 51.4 us; the launch traced here: 51.3 us
  Pallas kernels  50.5 us (98%)
  local copies, waits for them, and re-layouts  0.82 us (2%)
    pallas_call x1, Pallas kernels, by_kernel(): pl.pallas_call(functools.partial(triangle_kernel, layers, chips, count),...  50.5 us

profile of v8, /device:TPU:32, one launch (start us, length us, event | category | flops | bytes accessed | tf_op | source)
XLA Modules:
  0.0 51.3 jit_solution(11555845853343593989)
XLA Ops:
  0.0 50.5 %shard_map.73 = bf16[48,48,128]{2,1,0:T(8,128)(2,1)S(1)} custom-call(bf16[48,48,128]{2,1,0:T(8,128)(2,1)} %x_hbm.1, f32[128]{0:T(128)} %in_gain_hbm.1, bf16[128,128]{1,0:T(8,128)(2,1)} %left_weight_hbm.1, bf16[128,128]{1,0:T(8,128)(2,1)} %right_weight_hbm.1, f32[128]{0:T(128)} %mid_gain_hbm.1, bf16[128,128]{1,0:T(8,128)(2,1)} %out_weight_hbm.1, ...), custom_call_target="tpu_custom_call" | custom-call | tf_op jit(solution)/shard_map/pallas_call | solution.py:397
  50.5 0.8 %copy.9 = bf16[48,48,128]{2,1,0:T(8,128)(2,1)} copy(bf16[48,48,128]{2,1,0:T(8,128)(2,1)S(1)} %shard_map.73) | data formatting | bytes 1179648

commit v9 on v8

--- a/solution.py
+++ b/solution.py
@@ -227,11 +227,11 @@
                 for h in range(parts):
                     lanes = slice(h * LANES, (h + 1) * LANES)
                     lines = turn_lanes([
-                        got_left[u, n, :, lanes].astype(F32) for n in range(layers)
+                        got_left[u, n, :, lanes] for n in range(layers)
                     ])
                     for n in range(UNIT):
                         at = (h * UNIT + n) * GROUP
-                        turn_ref[at : at + GROUP, :] = lines[n]
+                        turn_ref[at : at + GROUP, :] = lines[n].astype(F32)
                     for d in range(GROUP):
                         line = turn_ref[pl.ds(h * UNIT * GROUP + d, UNIT, stride=GROUP), :]
                         near_left[u, d, :, lanes] = line.astype(BF16)
@@ -313,11 +313,11 @@
                     turn_ref[d * GROUP : (d + 1) * GROUP, :] = mix_recv[at, d].astype(F32)
                 for e in range(halves):
                     lines = turn_lanes([
-                        turn_ref[pl.ds(e * layers + n, GROUP, stride=GROUP), :]
+                        turn_ref[pl.ds(e * layers + n, GROUP, stride=GROUP), :].astype(BF16)
                         for n in range(layers)
                     ])
                     for n in range(layers):
-                        back_send[at, n, :, e * LANES : (e + 1) * LANES] = lines[n].astype(BF16)
+                        back_send[at, n, :, e * LANES : (e + 1) * LANES] = lines[n]
         send_back(g, range(layers // 2))
         back_recv[span, z] = back_send[span, z]
 

time: 51.4 us -> 51.2 us (level)
  no operation moved by 1% of the time
where the time goes in v9:
time: 51.2 us
  Pallas kernels  50.3 us (98%)
  local copies, waits for them, and re-layouts  0.82 us (2%)
    pallas_call x1, Pallas kernels, by_kernel(): pl.pallas_call(functools.partial(triangle_kernel, layers, chips, count),...  50.3 us

profile of v9, /device:TPU:32, one launch (start us, length us, event | category | flops | bytes accessed | tf_op | source)
XLA Modules:
  0.0 51.2 jit_solution(8018038303018700647)
XLA Ops:
  0.0 50.3 %shard_map.73 = bf16[48,48,128]{2,1,0:T(8,128)(2,1)S(1)} custom-call(bf16[48,48,128]{2,1,0:T(8,128)(2,1)} %x_hbm.1, f32[128]{0:T(128)} %in_gain_hbm.1, bf16[128,128]{1,0:T(8,128)(2,1)} %left_weight_hbm.1, bf16[128,128]{1,0:T(8,128)(2,1)} %right_weight_hbm.1, f32[128]{0:T(128)} %mid_gain_hbm.1, bf16[128,128]{1,0:T(8,128)(2,1)} %out_weight_hbm.1, ...), custom_call_target="tpu_custom_call" | custom-call | tf_op jit(solution)/shard_map/pallas_call | solution.py:397
  50.3 0.8 %copy.9 = bf16[48,48,128]{2,1,0:T(8,128)(2,1)} copy(bf16[48,48,128]{2,1,0:T(8,128)(2,1)S(1)} %shard_map.73) | data formatting | bytes 1179648

commit v10 on v9

--- a/solution.py
+++ b/solution.py
@@ -21,7 +21,7 @@
 BLOCKS = ((0, 1), (1, 1), (2, 1), (3, 1), (4, 1), (5, 1), (6, 3))
 PLAN = (
     "a0", "a1", "r0", "r1", "a2", "r2", "a3", "f0", "f1", "a4", "f2", "a5", "f3", "f4",
-    "m0", "m1", "f5", "m2", "m3", "m4", "m5", "c0", "c1", "h0", "c2", "h1", "m6", "c3",
+    "m0", "m1", "f5", "m2", "m3", "m4", "c0", "m5", "c1", "h0", "c2", "h1", "m6", "c3",
     "h2", "c4", "c5", "h3", "d0", "d1", "h4", "c6", "h5", "h6", "d2", "d3", "d4", "d5",
     "d6",
 )

time: 51.2 us -> 51 us (level)
  the two profiles are of different devices: /device:TPU:32 before, /device:TPU:1 now
where the time goes in v10:
time: 51 us; the launch traced here: 50.2 us
  Pallas kernels  49.4 us (97%)
  local copies, waits for them, and re-layouts  0.82 us (2%)
    pallas_call x1, Pallas kernels, by_kernel(): pl.pallas_call(functools.partial(triangle_kernel, layers, chips, count),...  49.4 us

profile of v10, /device:TPU:1, one launch (start us, length us, event | category | flops | bytes accessed | tf_op | source)
XLA Modules:
  0.0 50.2 jit_solution(5273037521220234061)
XLA Ops:
  0.0 49.4 %shard_map.73 = bf16[48,48,128]{2,1,0:T(8,128)(2,1)S(1)} custom-call(bf16[48,48,128]{2,1,0:T(8,128)(2,1)} %x_hbm.1, f32[128]{0:T(128)} %in_gain_hbm.1, bf16[128,128]{1,0:T(8,128)(2,1)} %left_weight_hbm.1, bf16[128,128]{1,0:T(8,128)(2,1)} %right_weight_hbm.1, f32[128]{0:T(128)} %mid_gain_hbm.1, bf16[128,128]{1,0:T(8,128)(2,1)} %out_weight_hbm.1, ...), custom_call_target="tpu_custom_call" | custom-call | tf_op jit(solution)/shard_map/pallas_call | solution.py:397
  49.4 0.8 %copy.9 = bf16[48,48,128]{2,1,0:T(8,128)(2,1)} copy(bf16[48,48,128]{2,1,0:T(8,128)(2,1)S(1)} %shard_map.73) | data formatting | bytes 1179648
